TPU v7x, 256 devices: a whole 4x4x8 slice. The times are simulated.
256 devices in a mesh: row: 16 (over y, x), col: 16 (over z, core).
Axes of the slice: x: 4, y: 4, z: 8, core: 2. Of those that a mesh axis runs over, the one named last changes fastest.
Arguments:
- tokens: bfloat16 [256, 16384], P('row', 'col'), may hold values from -6 to 6
- grad_out: bfloat16 [256, 16384], P('row', 'col'), may hold values from -6 to 6
- w_gate: bfloat16 [16384, 26624], P('col', 'row'), may hold values from -0.046875 to 0.046875
- w_up: bfloat16 [16384, 26624], P('col', 'row'), may hold values from -0.046875 to 0.046875
- w_down: bfloat16 [26624, 16384], P('row', 'col'), may hold values from -0.0390625 to 0.0390625
- radius: float32 [1], replicated, may hold values from 8 to 24
Outputs:
- perturbed_out: bfloat16 [256, 16384], P('row', 'col')
- grad_norm: float32 [1], replicated
All inputs are finite; a program needn't handle non-finite values.
Results may differ from a plain program's by a relative error of at most 0.02.
Values may be sent and summed in bfloat16 or wider, within the bound.
No kernel may reach another device: no remote copies, remote signals or barrier semaphores. Data moves between devices by JAX's collectives and lax.ppermute only.
A program may use at most 128 MiB of HBM per device.

v0:
```python
import jax
import jax.numpy as jnp
from jax import lax
from jax.experimental import pallas as pl
from jax.experimental.pallas import tpu as pltpu
from jax.sharding import Mesh
from jax.sharding import PartitionSpec as P

ROW = ("row_0", "row_1")
COL = ("col_0", "col_1")
Z = "col_0"
CORE = "col_1"
F32 = jnp.float32
BF16 = jnp.bfloat16
LANES = 128
SUBLANES = 8
MIB = 1 << 20
VMEM = pl.BlockSpec(memory_space=pltpu.VMEM)
SMEM = pl.BlockSpec(memory_space=pltpu.SMEM)


def dot(left, right, over):
    return lax.dot_general(
        left, right, (((over[0],), (over[1],)), ((), ())), preferred_element_type=F32
    )


def exchange(x, axis):
    return lax.all_to_all(x, axis, 0, 0, tiled=True)


def swap_cores(x):
    return lax.ppermute(x, CORE, [(0, 1), (1, 0)])


def local_kernel(body, out_shape, operands, limit=16, flops=1_000_000):
    return pl.pallas_call(
        body,
        in_specs=[SMEM if a.dtype == jnp.int32 else VMEM for a in operands],
        out_specs=[VMEM] * len(out_shape),
        out_shape=[jax.ShapeDtypeStruct(*shape) for shape in out_shape],
        compiler_params=pltpu.CompilerParams(vmem_limit_bytes=limit * MIB),
        cost_estimate=pl.CostEstimate(flops=flops, bytes_accessed=1_000_000, transcendentals=0),
    )(*operands)


def copies_in_kernel(tokens_ref, dy_ref, out_ref, done):
    rows = tokens_ref.shape[0]
    copies = [
        pltpu.make_async_copy(
            own_ref, out_ref.at[peer, kind * rows : (kind + 1) * rows], done.at[peer, kind]
        )
        for peer in range(out_ref.shape[0])
        for kind, own_ref in enumerate((tokens_ref, dy_ref))
    ]
    for copy in copies:
        copy.start()
    for copy in copies:
        copy.wait()


def copies_in(tokens, grad_out, sources):
    rows, depth = tokens.shape
    return pl.pallas_call(
        copies_in_kernel,
        in_specs=[pl.BlockSpec(memory_space=pl.ANY)] * 2,
        out_specs=VMEM,
        out_shape=jax.ShapeDtypeStruct((sources, 2 * rows, depth), BF16),
        scratch_shapes=[pltpu.SemaphoreType.DMA((sources, 2))],
        cost_estimate=pl.CostEstimate(flops=1_000_000, bytes_accessed=1_000_000, transcendentals=0),
        name="copies_in",
    )(tokens, grad_out)


def terms_kernel(
    core_ref, in_ref, wg_ref, wu_ref, wd_ref, theirs_ref, mine_ref, ord_ref, prod_ref, w_ref, down_ref, arrived
):
    j = pl.program_id(0)
    steps = w_ref.shape[0]
    peers = theirs_ref.shape[0]
    sources, rows2, depth = in_ref.shape
    rows = rows2 // 2
    tokens = sources * rows
    half = tokens // 2
    slab = tokens // peers
    part = LANES // peers
    width = steps * part
    core = core_ref[0]
    sides = ((1 - core, theirs_ref), (core, mine_ref))

    def fetch(step, kind):
        at = pl.multiple_of(step * LANES, LANES)
        if kind == 2:
            source, target = wd_ref.at[pl.ds(at, LANES)], down_ref.at[pl.ds(at, LANES)]
        else:
            source = (wg_ref, wu_ref)[kind].at[:, pl.ds(at, LANES)]
            target = w_ref.at[step, :, pl.ds(kind * LANES, LANES)]
        return pltpu.make_async_copy(source, target, arrived.at[step, kind])

    @pl.when(j == 0)
    def _():
        for step in range(steps):
            fetch(step, 0).start()
            fetch(step, 1).start()
        for step in range(steps):
            fetch(step, 2).start()
        for kind in range(2):
            row_at = 2 * width + kind * slab
            a = in_ref[:, kind * rows : (kind + 1) * rows, :].reshape(tokens, depth)
            for side, out_ref in sides:
                own = in_ref[
                    pl.ds(side * (sources // 2), sources // 2), kind * rows : (kind + 1) * rows, :
                ].reshape(half, depth)
                gram = dot(a, own, (1, 1)).astype(BF16)
                out_ref[:, row_at : row_at + slab, :] = gram.reshape(peers, slab, half)
        for at, side in ((0, 1 - core), (half, core)):
            own = in_ref[pl.ds(side * (sources // 2), sources // 2), rows:, :]
            ord_ref[at : at + half] = own.reshape(half, depth)

    last = pl.multiple_of(jnp.maximum(j - 1, 0) * part, part)
    for side, out_ref in sides:
        token_at = pl.multiple_of(side * half, half)
        block = prod_ref[lax.rem(j + 1, 2), pl.ds(token_at, half), :].T.astype(BF16)
        out_ref[:, pl.ds(last, part), :] = block[:LANES].reshape(peers, part, half)
        out_ref[:, pl.ds(width + last, part), :] = block[LANES:].reshape(peers, part, half)
    x = in_ref[:, :rows, :].reshape(tokens, depth)
    now = jnp.minimum(j, steps - 1)

    @pl.when(j < steps)
    def _():
        fetch(now, 0).wait()
        fetch(now, 1).wait()

    prod_ref[lax.rem(j, 2)] = jnp.dot(x, w_ref[now], preferred_element_type=F32)

    @pl.when(j == steps)
    def _():
        for step in range(steps):
            fetch(step, 2).wait()
        for first in range(0, steps, 4):
            end = min(first + 4, steps)
            rows_in = slice(first * LANES, end * LANES)
            block = dot(down_ref[rows_in], ord_ref[...], (1, 1)).astype(BF16)
            for step in range(first, end):
                piece = block[(step - first) * LANES : (step - first + 1) * LANES]
                piece = piece.reshape(peers, part, tokens)
                to = 2 * width + 2 * slab + step * part
                theirs_ref[:, to : to + part, :] = piece[:, :, :half]
                mine_ref[:, to : to + part, :] = piece[:, :, half:]


def terms(core, fetched, w_gate, w_up, w_down, peers):
    depth, hidden = w_gate.shape
    tokens = fetched.shape[0] * fetched.shape[1] // 2
    steps = hidden // LANES
    rows = 3 * hidden // peers + 2 * tokens // peers
    out = jax.ShapeDtypeStruct((peers, rows, tokens // 2), BF16)
    dy = jax.ShapeDtypeStruct((tokens, depth), BF16)
    whole = pl.BlockSpec(out.shape, lambda j: (0, 0, 0))
    hbm = pl.BlockSpec(memory_space=pl.ANY)
    return pl.pallas_call(
        terms_kernel,
        grid=(steps + 1,),
        in_specs=[SMEM, pl.BlockSpec(fetched.shape, lambda j: (0, 0, 0)), hbm, hbm, hbm],
        out_specs=[whole, whole, pl.BlockSpec(dy.shape, lambda j: (0, 0))],
        out_shape=[out, out, dy],
        scratch_shapes=[
            pltpu.VMEM((2, tokens, 2 * LANES), F32),
            pltpu.VMEM((steps, depth, 2 * LANES), BF16),
            pltpu.VMEM((hidden, depth), BF16),
            pltpu.SemaphoreType.DMA((steps, 3)),
        ],
        compiler_params=pltpu.CompilerParams(vmem_limit_bytes=TERMS_MIB * MIB),
        cost_estimate=pl.CostEstimate(
            flops=6 * tokens * depth * hidden, bytes_accessed=6 * depth * hidden, transcendentals=0
        ),
        name="terms",
    )(core, fetched, w_gate, w_up, w_down)


def add_kernel(a_ref, b_ref, first_ref, second_ref):
    rows = first_ref.shape[1]
    both = (a_ref[...].astype(F32) + b_ref[...].astype(F32)).astype(BF16)
    first_ref[...] = both[:, :rows]
    second_ref[...] = both[:, rows:]


def middle_kernel(sums_ref, grad_ref, sent_ref, gate_ref, up_ref):
    peers, _, _ = sums_ref.shape
    width = grad_ref.shape[1]
    total = sums_ref[0].astype(F32)
    for peer in range(1, peers):
        total = total + sums_ref[peer].astype(F32)
    gate_ref[...] = total[:width]
    up_ref[...] = total[width : 2 * width]
    grams = total[2 * width :].astype(BF16)
    sent_ref[:, :width, :] = grad_ref[...]
    for peer in range(peers):
        sent_ref[peer, width:, :] = grams


def acts_kernel(sums_ref, gate_ref, up_ref, acts_ref):
    width = gate_ref.shape[0]
    total = sums_ref[0, :width].astype(F32)
    for peer in range(1, sums_ref.shape[0]):
        total = total + sums_ref[peer, :width].astype(F32)
    grad_hidden = total.astype(BF16).astype(F32)
    gate, up = gate_ref[...], up_ref[...]
    sig = jax.nn.sigmoid(gate)
    silu = gate * sig
    acts_ref[:width] = (grad_hidden * up * sig * (1.0 + gate * (1.0 - sig))).astype(BF16)
    acts_ref[width : 2 * width] = (grad_hidden * silu).astype(BF16)
    acts_ref[2 * width :] = (silu * up).astype(BF16)


def step_kernel(core_ref, acts_ref, arrived_ref, grams_ref, step_ref, local_ref):
    peers, rows, half = grams_ref.shape
    width = acts_ref.shape[0] // 3
    slab = (rows - width) // 2
    core = core_ref[0]
    kinds = ((0, 2 * width, width), (2 * width, 3 * width, width + slab))
    local = 0.0
    for first, end, at in kinds:
        product = 0.0
        for side, part_ref in ((1 - core, arrived_ref), (core, acts_ref)):
            gram = grams_ref[pl.ds(side * (peers // 2), peers // 2), at : at + slab, :]
            product += dot(part_ref[first:end], gram.reshape(half, half), (1, 0))
        local += jnp.sum(acts_ref[first:end].astype(F32) * product)
        if first == 0:
            step_ref[...] = product
    local_ref[...] = jnp.full(local_ref.shape, local, F32)


def norm_kernel(plane_ref, acts_ref, out_ref):
    peers, _, _ = out_ref.shape
    width = acts_ref.shape[0] // 3
    plane = plane_ref[0]
    for peer in range(1, plane_ref.shape[0]):
        plane = plane + plane_ref[peer]
    high = plane.astype(BF16).astype(F32)
    pair = jnp.concatenate([high, plane - high], 0).astype(BF16)
    hidden = acts_ref[2 * width :]
    for peer in range(peers):
        out_ref[peer, :width] = hidden
        out_ref[peer, width:] = pair


def pert_kernel(ends_ref, gate_ref, up_ref, step_ref, radius_ref, out_ref, scale_ref, norm_ref):
    peers, _, lanes = ends_ref.shape
    width = gate_ref.shape[0]
    total = jnp.zeros((SUBLANES, lanes), F32)
    for peer in range(peers):
        pair = ends_ref[peer, width:].astype(F32)
        total = total + (pair[:SUBLANES] + pair[SUBLANES:])
    scale = radius_ref[...] * lax.rsqrt(total + 1e-06)
    norm_ref[...] = jnp.sqrt(total)
    scale_ref[...] = scale
    pgate = gate_ref[...] + scale[:1] * step_ref[:width]
    pup = up_ref[...] + scale[:1] * step_ref[width:]
    phidden = (pgate * jax.nn.sigmoid(pgate) * pup).astype(BF16)
    for peer in range(peers):
        out_ref[peer] = phidden


def out_kernel(
    core_ref, scale_ref, pt_ref, pm_ref, ht_ref, hm_ref, wd_ref, dy_ref, out_ref, ph_ref, mix_ref
):
    peers, width, half = pm_ref.shape
    part = LANES // peers

    @pl.when(pl.program_id(0) == 0)
    def _():
        for at, p_ref in ((0, pt_ref), (half, pm_ref)):
            for j in range(width // part):
                block = p_ref[:, j * part : (j + 1) * part, :].reshape(LANES, half)
                ph_ref[at : at + half, j * LANES : (j + 1) * LANES] = (
                    block.astype(F32).T.astype(BF16)
                )
        for a, p_ref in ((0, pt_ref), (half, pm_ref)):
            for b, h_ref in ((0, ht_ref), (half, hm_ref)):
                p = p_ref[...].reshape(peers * width, half)
                h = h_ref[:, :width, :].reshape(peers * width, half)
                mix = scale_ref[:1] * dot(p, h, (0, 0))
                mix_ref[a : a + half, b : b + half] = mix.astype(BF16)

    acc = dot(ph_ref[...], wd_ref[...], (1, 0)) + dot(mix_ref[...], dy_ref[...], (1, 0))
    out = acc.astype(BF16)
    theirs = pl.multiple_of((1 - core_ref[0]) * half, half)
    mine = pl.multiple_of(core_ref[0] * half, half)
    out_ref[pl.ds(theirs, half), :] = out[:half]
    out_ref[pl.ds(mine, half), :] = out[half:]


def out_terms(core, scale, ph_theirs, ph_mine, h_theirs, h_mine, w_down, dy):
    hidden, depth = w_down.shape
    tokens = dy.shape[0]
    block = min(depth, 256)
    ph_spec = pl.BlockSpec(ph_mine.shape, lambda n: (0, 0, 0))
    h_spec = pl.BlockSpec(h_mine.shape, lambda n: (0, 0, 0))
    return pl.pallas_call(
        out_kernel,
        grid=(depth // block,),
        in_specs=[
            SMEM,
            pl.BlockSpec(scale.shape, lambda n: (0, 0)),
            ph_spec,
            ph_spec,
            h_spec,
            h_spec,
            pl.BlockSpec((hidden, block), lambda n: (0, n)),
            pl.BlockSpec((tokens, block), lambda n: (0, n)),
        ],
        out_specs=pl.BlockSpec((tokens, block), lambda n: (0, n)),
        out_shape=jax.ShapeDtypeStruct((tokens, depth), BF16),
        scratch_shapes=[pltpu.VMEM((tokens, hidden), BF16), pltpu.VMEM((tokens, tokens), BF16)],
        compiler_params=pltpu.CompilerParams(vmem_limit_bytes=24 * MIB),
        cost_estimate=pl.CostEstimate(
            flops=2 * tokens * depth * hidden, bytes_accessed=2 * depth * hidden, transcendentals=0
        ),
        name="out_terms",
    )(core, scale, ph_theirs, ph_mine, h_theirs, h_mine, w_down, dy)


def per_device(tokens, grad_out, w_gate, w_up, w_down, radius):
    core = lax.axis_index(CORE).reshape(1).astype(jnp.int32)
    peers = lax.axis_size(Z)
    sources = lax.axis_size(ROW)
    rows, depth = tokens.shape
    half = sources * rows // 2
    width = w_gate.shape[1] // peers
    slab = 2 * half // peers

    radius = jnp.broadcast_to(radius, (SUBLANES, half))
    tokens, grad_out, core, radius = lax.optimization_barrier(
        (tokens, grad_out, core, radius)
    )
    fetched = exchange(copies_in(tokens, grad_out, sources), ROW)
    theirs, mine, dy = terms(core, fetched, w_gate, w_up, w_down, peers)
    arrived = swap_cores(theirs)
    chip, chip_gh = local_kernel(
        add_kernel,
        [((peers, 2 * (width + slab), half), BF16), ((peers, width, half), BF16)],
        (mine, arrived),
    )
    sums = exchange(chip, Z)
    sent, gate, up = local_kernel(
        middle_kernel,
        [
            ((peers, width + 2 * slab, half), BF16),
            ((width, half), F32),
            ((width, half), F32),
        ],
        (sums, chip_gh),
    )
    sums = exchange(sent, Z)
    (acts,) = local_kernel(acts_kernel, [((3 * width, half), BF16)], (sums, gate, up))
    arrived = swap_cores(acts)
    step, local = local_kernel(
        step_kernel,
        [((2 * width, half), F32), ((2 * sources, SUBLANES, LANES), F32)],
        (core, acts, arrived, sums),
    )
    plane = exchange(local, (*ROW, CORE))
    (sent,) = local_kernel(
        norm_kernel, [((peers, width + 2 * SUBLANES, half), BF16)], (plane, acts)
    )
    h_mine = exchange(sent, Z)
    tile = ((SUBLANES, half), F32)
    sent, scale, norm = local_kernel(
        pert_kernel, [((peers, width, half), BF16), tile, tile], (h_mine, gate, up, step, radius)
    )
    ph_mine = exchange(sent, Z)
    ph_mine, h_mine = lax.optimization_barrier((ph_mine, h_mine))
    ph_theirs = swap_cores(ph_mine)
    h_theirs = swap_cores(h_mine)
    partial_out = out_terms(core, scale, ph_theirs, ph_mine, h_theirs, h_mine, w_down, dy)
    partial_out, norm = lax.optimization_barrier((partial_out, norm[0, :1]))
    parts = exchange(partial_out.reshape(sources, rows, depth), ROW)
    return (jnp.sum(parts.astype(F32), 0).astype(BF16), norm)


TERMS_MIB = 60


def solution(mesh):
    split = Mesh(mesh.devices.reshape(4, 4, 8, 2), ("row_0", "row_1", "col_0", "col_1"))
    return jax.shard_map(
        per_device,
        mesh=split,
        in_specs=(P(ROW, COL), P(ROW, COL), P(COL, ROW), P(COL, ROW), P(ROW, COL), P()),
        out_specs=(P(ROW, COL), P()),
        check_vma=False,
    )
```

profile of v0, /device:TPU:1, one launch (start us, length us, event | category | flops | bytes accessed | tf_op | source)
XLA Modules:
  0.0 172.3 jit_solution(4087862858285564726)
XLA Ops:
  1.3 2.6 %copies_in.1 = bf16[16,32,1024]{2,1,0:T(8,128)(2,1)} custom-call(bf16[16,1024]{1,0:T(8,128)(2,1)} %tokens_ref, bf16[16,1024]{1,0:T(8,128)(2,1)} %dy_ref), custom_call_target="tpu_custom_call" | custom-call | flops 1000000 | bytes 1000000 | tf_op jit(solution)/shard_map/copies_in/pallas_call | solution.py:64
  3.9 23.7 %all_to_all.35.in_ref = bf16[16,32,1024]{2,1,0:T(8,128)(2,1)} all-to-all(bf16[16,32,1024]{2,1,0:T(8,128)(2,1)} %copies_in.1), channel_id=1, replica_groups=mesh['row_0'=4,'row_1'=4,'col_0'=8,'col_1'=2] {'row_0','row_1'}, dimensions={0} | all-to-all | bytes 2097152 | tf_op jit(solution)/shard_map/all_to_all | solution.py:29
  27.6 11.5 %terms.1 = (bf16[8,688,128]{2,1,0:T(8,128)(2,1)}, bf16[8,688,128]{2,1,0:T(8,128)(2,1)}, bf16[256,1024]{1,0:T(8,128)(2,1)}) custom-call(s32[1]{0:T(128)} %bitcast.core_ref, bf16[16,32,1024]{2,1,0:T(8,128)(2,1)} %all_to_all.35.in_ref, bf16[1024,1664]{1,0:T(8,128)(2,1)} %wg_ref.1, bf16[1024,1664]{1,0:T(8,128)(2,1)} %wu_ref.1, bf16[1664,1024]{1,0:T(8,128)(2,1)} %wd_ref.3), custom_call_target="tpu_custom_call" | custom-call | flops 2617245696 | bytes 10223616 | tf_op jit(solution)/shard_map/terms/pallas_call | solution.py:161
  39.2 2.2 %collective-permute-start = (bf16[8,688,128]{2,1,0:T(8,128)(2,1)}, bf16[8,688,128]{2,1,0:T(8,128)(2,1)S(1)}, u32[]{:S(2)}, u32[]{:S(2)}) collective-permute-start(bf16[8,688,128]{2,1,0:T(8,128)(2,1)} %get-tuple-element.27), channel_id=1, source_target_pairs={{0,1},{1,0},{2,3},{3,2},{4,5},{5,4},{6,7},{7,6},{8,9},{9,8},{10,11... | collective-permute-start | bytes 4227080 | tf_op jit(solution)/shard_map/ppermute | solution.py:33
  41.3 3.0 %collective-permute-done.b_ref = bf16[8,688,128]{2,1,0:T(8,128)(2,1)S(1)} collective-permute-done((bf16[8,688,128]{2,1,0:T(8,128)(2,1)}, bf16[8,688,128]{2,1,0:T(8,128)(2,1)S(1)}, u32[]{:S(2)}, u32[]{:S(2)}) %collective-permute-start) | collective-permute-done | bytes 1409056 | tf_op jit(solution)/shard_map/ppermute | solution.py:33
  44.3 0.0 copy-start.1
  44.3 1.3 copy-done.1
  45.7 0.3 shard_map.80
  46.0 34.5 %all_to_all.36.sums_ref = bf16[8,480,128]{2,1,0:T(8,128)(2,1)S(1)} all-to-all(bf16[8,480,128]{2,1,0:T(8,128)(2,1)S(1)} %get-tuple-element.28), channel_id=1, replica_groups=mesh['row_0'=4,'row_1'=4,'col_0'=8,'col_1'=2] {'col_0'}, dimensions={0} | all-to-all | bytes 1966080 | tf_op jit(solution)/shard_map/all_to_all | solution.py:29
  80.5 0.1 shard_map.81
  80.6 0.0 copy-start
  80.6 0.0 copy-start.2
  80.6 18.1 %all_to_all.37.sums_ref.grams_ref = bf16[8,272,128]{2,1,0:T(8,128)(2,1)S(1)} all-to-all(bf16[8,272,128]{2,1,0:T(8,128)(2,1)S(1)} %get-tuple-element.30), channel_id=1, replica_groups=mesh['row_0'=4,'row_1'=4,'col_0'=8,'col_1'=2] {'col_0'}, dimensions={0} | all-to-all | bytes 1114112 | tf_op jit(solution)/shard_map/all_to_all | solution.py:29
  98.7 0.1 shard_map.82.acts_ref
  98.9 3.8 %collective-permute-start.1 = (bf16[624,128]{1,0:T(8,128)(2,1)S(1)}, bf16[624,128]{1,0:T(8,128)(2,1)S(1)}, u32[]{:S(2)}, u32[]{:S(2)}) collective-permute-start(bf16[624,128]{1,0:T(8,128)(2,1)S(1)} %shard_map.82.acts_ref), channel_id=1, source_target_pairs={{0,1},{1,0},{2,3},{3,2},{4,5},{5,4},{6,7},{7,6},{8,9},{9,8},{10,11... | collective-permute-start | bytes 479240 | tf_op jit(solution)/shard_map/ppermute | solution.py:33
  102.6 1.0 collective-permute-done.1.arrived_ref
  103.6 0.4 shard_map.83
  104.0 11.0 %all_to_all.38.plane_ref = f32[32,8,128]{2,1,0:T(8,128)S(1)} all-to-all(f32[32,8,128]{2,1,0:T(8,128)S(1)} %get-tuple-element.33), channel_id=1, replica_groups=mesh['row_0'=4,'row_1'=4,'col_0'=8,'col_1'=2] {'row_0','row_1','col_1'}, dimensions={0} | all-to-all | bytes 262144 | tf_op jit(solution)/shard_map/all_to_all | solution.py:29
  115.0 0.1 shard_map.84
  115.1 18.9 %all_to_all.39.ends_ref.hm_ref = bf16[8,224,128]{2,1,0:T(8,128)(2,1)S(1)} all-to-all(bf16[8,224,128]{2,1,0:T(8,128)(2,1)S(1)} %shard_map.84), channel_id=1, replica_groups=mesh['row_0'=4,'row_1'=4,'col_0'=8,'col_1'=2] {'col_0'}, dimensions={0} | all-to-all | bytes 917504 | tf_op jit(solution)/shard_map/all_to_all | solution.py:29
  134.0 0.1 shard_map.85
  134.0 17.3 %all_to_all.40.pm_ref = bf16[8,208,128]{2,1,0:T(8,128)(2,1)S(1)} all-to-all(bf16[8,208,128]{2,1,0:T(8,128)(2,1)S(1)} %get-tuple-element.37), channel_id=1, replica_groups=mesh['row_0'=4,'row_1'=4,'col_0'=8,'col_1'=2] {'col_0'}, dimensions={0} | all-to-all | bytes 851968 | tf_op jit(solution)/shard_map/all_to_all | solution.py:29
  151.3 1.5 collective-permute-start.3
  152.8 0.0 collective-permute-start.2
  152.8 0.5 slice.3
  153.3 1.5 collective-permute-done.2.pt_ref
  154.8 0.0 collective-permute-done.3.ht_ref
  154.8 0.0 copy-done
  154.8 0.0 copy-done.2
  154.8 3.3 %out_terms.1 = bf16[256,1024]{1,0:T(8,128)(2,1)S(1)} custom-call(s32[1]{0:T(128)} %bitcast.core_ref, f32[8,128]{1,0:T(8,128)S(1)} %get-tuple-element.36.scale_ref, bf16[8,208,128]{2,1,0:T(8,128)(2,1)S(1)} %collective-permute-done.2.pt_ref, bf16[8,208,128]{2,1,0:T(8,128)(2,1)S(1)} %all_to_all.40.pm_ref, ...), custom_call_target="tpu_custom_call" | custom-call | flops 872415232 | bytes 3407872 | tf_op jit(solution)/shard_map/out_terms/pallas_call | solution.py:300
  158.1 13.5 %all_to_all.41 = bf16[16,16,1024]{2,1,0:T(8,128)(2,1)S(1)} all-to-all(bf16[16,16,1024]{2,1,0:T(8,128)(2,1)S(1)} %bitcast.5), channel_id=1, replica_groups=mesh['row_0'=4,'row_1'=4,'col_0'=8,'col_1'=2] {'row_0','row_1'}, dimensions={0} | all-to-all | bytes 1048576 | tf_op jit(solution)/shard_map/all_to_all | solution.py:29
  171.6 0.7 reduce_sum.12
  (1 shorter events, 0.0 us)
Async XLA Ops:
  39.2 5.2 %collective-permute-start = (bf16[8,688,128]{2,1,0:T(8,128)(2,1)}, bf16[8,688,128]{2,1,0:T(8,128)(2,1)S(1)}, u32[]{:S(2)}, u32[]{:S(2)}) collective-permute-start(bf16[8,688,128]{2,1,0:T(8,128)(2,1)} %get-tuple-element.27), channel_id=1, source_target_pairs={{0,1},{1,0},{2,3},{3,2},{4,5},{5,4},{6,7},{7,6},{8,9},{9,8},{10,11... | collective-permute-start | bytes 4227080 | tf_op jit(solution)/shard_map/ppermute | solution.py:33
  44.3 1.4 copy-start.1
  80.6 74.2 %copy-start = (bf16[1664,1024]{1,0:T(8,128)(2,1)S(1)}, bf16[1664,1024]{1,0:T(8,128)(2,1)}, u32[]{:S(2)}) copy-start(bf16[1664,1024]{1,0:T(8,128)(2,1)} %wd_ref.3) | copy-start | bytes 10223620
  80.6 74.2 %copy-start.2 = (bf16[256,1024]{1,0:T(8,128)(2,1)S(1)}, bf16[256,1024]{1,0:T(8,128)(2,1)}, u32[]{:S(2)}) copy-start(bf16[256,1024]{1,0:T(8,128)(2,1)} %get-tuple-element.40.dy_ref) | copy-start | bytes 1572868
  98.9 4.8 %collective-permute-start.1 = (bf16[624,128]{1,0:T(8,128)(2,1)S(1)}, bf16[624,128]{1,0:T(8,128)(2,1)S(1)}, u32[]{:S(2)}, u32[]{:S(2)}) collective-permute-start(bf16[624,128]{1,0:T(8,128)(2,1)S(1)} %shard_map.82.acts_ref), channel_id=1, source_target_pairs={{0,1},{1,0},{2,3},{3,2},{4,5},{5,4},{6,7},{7,6},{8,9},{9,8},{10,11... | collective-permute-start | bytes 479240 | tf_op jit(solution)/shard_map/ppermute | solution.py:33
  151.3 3.5 %collective-permute-start.3 = (bf16[8,224,128]{2,1,0:T(8,128)(2,1)S(1)}, bf16[8,224,128]{2,1,0:T(8,128)(2,1)S(1)}, u32[]{:S(2)}, u32[]{:S(2)}) collective-permute-start(bf16[8,224,128]{2,1,0:T(8,128)(2,1)S(1)} %all_to_all.39.ends_ref.hm_ref), channel_id=1, source_target_pairs={{0,1},{1,0},{2,3},{3,2},{4,5},{5,4},{6,7},{7,6},{8,9},{9,8},{10,11... | collective-permute-start | bytes 1376264 | tf_op jit(solution)/shard_map/ppermute | solution.py:33
  152.8 2.1 %collective-permute-start.2 = (bf16[8,208,128]{2,1,0:T(8,128)(2,1)S(1)}, bf16[8,208,128]{2,1,0:T(8,128)(2,1)S(1)}, u32[]{:S(2)}, u32[]{:S(2)}) collective-permute-start(bf16[8,208,128]{2,1,0:T(8,128)(2,1)S(1)} %all_to_all.40.pm_ref), channel_id=1, source_target_pairs={{0,1},{1,0},{2,3},{3,2},{4,5},{5,4},{6,7},{7,6},{8,9},{9,8},{10,11... | collective-permute-start | bytes 1277960 | tf_op jit(solution)/shard_map/ppermute | solution.py:33
where the time goes:
time: 173 us; the launch traced here: 172 us
  blocking collectives  137 us (79%)
  Pallas kernels  18.4 us (11%)
  starting transfers between devices  7.41 us (4%)
  waiting for transfers between devices  5.58 us (3%)
  local copies, waits for them, and re-layouts  1.87 us (1%)
    all_to_all x7, blocking collectives, exchange(): return lax.all_to_all(x, axis, 0, 0, tiled=True)  137 us
    pallas_call x1, Pallas kernels, terms(): pl.pallas_call(terms_kernel, grid=(steps + 1,), in_specs=[SMEM, pl.BlockS...  11.5 us
    ppermute x4, starting transfers between devices, swap_cores(): return lax.ppermute(x, CORE, [(0, 1), (1, 0)])  7.41 us
    ppermute x4, waiting for transfers between devices, swap_cores(): return lax.ppermute(x, CORE, [(0, 1), (1, 0)])  5.58 us
  transfers between devices with their start and end apart: 4, of which 3 were waited for; matrix products, arithmetic and copies ran while one was open for 0% of the time, Pallas kernels for 0%

commit v1 on v0

--- a/solution.py
+++ b/solution.py
@@ -48,15 +48,17 @@
     rows = tokens_ref.shape[0]
     copies = [
         pltpu.make_async_copy(
-            own_ref, out_ref.at[peer, kind * rows : (kind + 1) * rows], done.at[peer, kind]
+            own_ref, out_ref.at[0, kind * rows : (kind + 1) * rows], done.at[kind]
         )
-        for peer in range(out_ref.shape[0])
         for kind, own_ref in enumerate((tokens_ref, dy_ref))
     ]
     for copy in copies:
         copy.start()
     for copy in copies:
         copy.wait()
+    both = out_ref[0]
+    for peer in range(1, out_ref.shape[0]):
+        out_ref[peer] = both
 
 
 def copies_in(tokens, grad_out, sources):
@@ -66,17 +68,18 @@
         in_specs=[pl.BlockSpec(memory_space=pl.ANY)] * 2,
         out_specs=VMEM,
         out_shape=jax.ShapeDtypeStruct((sources, 2 * rows, depth), BF16),
-        scratch_shapes=[pltpu.SemaphoreType.DMA((sources, 2))],
-        cost_estimate=pl.CostEstimate(flops=1_000_000, bytes_accessed=1_000_000, transcendentals=0),
+        scratch_shapes=[pltpu.SemaphoreType.DMA((2,))],
+        compiler_params=pltpu.CompilerParams(vmem_limit_bytes=4 * MIB),
+        cost_estimate=pl.CostEstimate(flops=20_000_000_000, bytes_accessed=1_000_000, transcendentals=0),
         name="copies_in",
     )(tokens, grad_out)
 
 
 def terms_kernel(
-    core_ref, in_ref, wg_ref, wu_ref, wd_ref, theirs_ref, mine_ref, ord_ref, prod_ref, w_ref, down_ref, arrived
+    place_ref, in_ref, wg_ref, wu_ref, wd_ref, theirs_ref, mine_ref, ord_ref, prod_ref
 ):
     j = pl.program_id(0)
-    steps = w_ref.shape[0]
+    steps = wg_ref.shape[1] // LANES
     peers = theirs_ref.shape[0]
     sources, rows2, depth = in_ref.shape
     rows = rows2 // 2
@@ -85,25 +88,11 @@
     slab = tokens // peers
     part = LANES // peers
     width = steps * part
-    core = core_ref[0]
+    core = place_ref[0]
     sides = ((1 - core, theirs_ref), (core, mine_ref))
-
-    def fetch(step, kind):
-        at = pl.multiple_of(step * LANES, LANES)
-        if kind == 2:
-            source, target = wd_ref.at[pl.ds(at, LANES)], down_ref.at[pl.ds(at, LANES)]
-        else:
-            source = (wg_ref, wu_ref)[kind].at[:, pl.ds(at, LANES)]
-            target = w_ref.at[step, :, pl.ds(kind * LANES, LANES)]
-        return pltpu.make_async_copy(source, target, arrived.at[step, kind])
 
     @pl.when(j == 0)
     def _():
-        for step in range(steps):
-            fetch(step, 0).start()
-            fetch(step, 1).start()
-        for step in range(steps):
-            fetch(step, 2).start()
         for kind in range(2):
             row_at = 2 * width + kind * slab
             a = in_ref[:, kind * rows : (kind + 1) * rows, :].reshape(tokens, depth)
@@ -124,23 +113,16 @@
         out_ref[:, pl.ds(last, part), :] = block[:LANES].reshape(peers, part, half)
         out_ref[:, pl.ds(width + last, part), :] = block[LANES:].reshape(peers, part, half)
     x = in_ref[:, :rows, :].reshape(tokens, depth)
-    now = jnp.minimum(j, steps - 1)
-
-    @pl.when(j < steps)
-    def _():
-        fetch(now, 0).wait()
-        fetch(now, 1).wait()
-
-    prod_ref[lax.rem(j, 2)] = jnp.dot(x, w_ref[now], preferred_element_type=F32)
+    now = pl.multiple_of(jnp.minimum(j, steps - 1) * LANES, LANES)
+    w = jnp.concatenate([wg_ref[:, pl.ds(now, LANES)], wu_ref[:, pl.ds(now, LANES)]], 1)
+    prod_ref[lax.rem(j, 2)] = jnp.dot(x, w, preferred_element_type=F32)
 
     @pl.when(j == steps)
     def _():
-        for step in range(steps):
-            fetch(step, 2).wait()
         for first in range(0, steps, 4):
             end = min(first + 4, steps)
             rows_in = slice(first * LANES, end * LANES)
-            block = dot(down_ref[rows_in], ord_ref[...], (1, 1)).astype(BF16)
+            block = dot(wd_ref[rows_in], ord_ref[...], (1, 1)).astype(BF16)
             for step in range(first, end):
                 piece = block[(step - first) * LANES : (step - first + 1) * LANES]
                 piece = piece.reshape(peers, part, tokens)
@@ -149,76 +131,74 @@
                 mine_ref[:, to : to + part, :] = piece[:, :, half:]
 
 
-def terms(core, fetched, w_gate, w_up, w_down, peers):
+def terms(place, fetched, w_gate, w_up, w_down, peers):
     depth, hidden = w_gate.shape
     tokens = fetched.shape[0] * fetched.shape[1] // 2
     steps = hidden // LANES
     rows = 3 * hidden // peers + 2 * tokens // peers
     out = jax.ShapeDtypeStruct((peers, rows, tokens // 2), BF16)
     dy = jax.ShapeDtypeStruct((tokens, depth), BF16)
-    whole = pl.BlockSpec(out.shape, lambda j: (0, 0, 0))
-    hbm = pl.BlockSpec(memory_space=pl.ANY)
     return pl.pallas_call(
         terms_kernel,
         grid=(steps + 1,),
-        in_specs=[SMEM, pl.BlockSpec(fetched.shape, lambda j: (0, 0, 0)), hbm, hbm, hbm],
-        out_specs=[whole, whole, pl.BlockSpec(dy.shape, lambda j: (0, 0))],
+        in_specs=[SMEM] + [VMEM] * 4,
+        out_specs=[VMEM] * 3,
         out_shape=[out, out, dy],
-        scratch_shapes=[
-            pltpu.VMEM((2, tokens, 2 * LANES), F32),
-            pltpu.VMEM((steps, depth, 2 * LANES), BF16),
-            pltpu.VMEM((hidden, depth), BF16),
-            pltpu.SemaphoreType.DMA((steps, 3)),
-        ],
+        scratch_shapes=[pltpu.VMEM((2, tokens, 2 * LANES), F32)],
         compiler_params=pltpu.CompilerParams(vmem_limit_bytes=TERMS_MIB * MIB),
         cost_estimate=pl.CostEstimate(
             flops=6 * tokens * depth * hidden, bytes_accessed=6 * depth * hidden, transcendentals=0
         ),
         name="terms",
-    )(core, fetched, w_gate, w_up, w_down)
-
-
-def add_kernel(a_ref, b_ref, first_ref, second_ref):
-    rows = first_ref.shape[1]
-    both = (a_ref[...].astype(F32) + b_ref[...].astype(F32)).astype(BF16)
-    first_ref[...] = both[:, :rows]
-    second_ref[...] = both[:, rows:]
-
-
-def middle_kernel(sums_ref, grad_ref, sent_ref, gate_ref, up_ref):
-    peers, _, _ = sums_ref.shape
-    width = grad_ref.shape[1]
-    total = sums_ref[0].astype(F32)
-    for peer in range(1, peers):
-        total = total + sums_ref[peer].astype(F32)
-    gate_ref[...] = total[:width]
-    up_ref[...] = total[width : 2 * width]
-    grams = total[2 * width :].astype(BF16)
-    sent_ref[:, :width, :] = grad_ref[...]
-    for peer in range(peers):
-        sent_ref[peer, width:, :] = grams
-
-
-def acts_kernel(sums_ref, gate_ref, up_ref, acts_ref):
+    )(place, fetched, w_gate, w_up, w_down)
+
+
+def split_kernel(place_ref, mine_ref, arrived_ref, first_ref, second_ref, keep_ref):
+    parity = lax.rem(place_ref[1], 2)
+    cut = first_ref.shape[1]
+    for q in range(keep_ref.shape[0]):
+        away, here = 2 * q + 1 - parity, 2 * q + parity
+        sent = (mine_ref[away].astype(F32) + arrived_ref[away].astype(F32)).astype(BF16)
+        first_ref[q] = sent[:cut]
+        second_ref[q] = sent[cut:]
+        keep_ref[q] = mine_ref[here].astype(F32) + arrived_ref[here].astype(F32)
+
+
+def pair_kernel(place_ref, keep_ref, first_ref, second_ref, own_ref, up_ref, down_ref, far_ref):
+    count = keep_ref.shape[0]
+    cut = first_ref.shape[1]
+    q0 = place_ref[1] // 2
+    for shift, out_ref in ((0, own_ref), (1, up_ref), (count - 1, down_ref), (2, far_ref)):
+        q = lax.rem(q0 + shift, count)
+        out_ref[:cut] = (keep_ref[q, :cut] + first_ref[q].astype(F32)).astype(out_ref.dtype)
+        out_ref[cut:] = (keep_ref[q, cut:] + second_ref[q].astype(F32)).astype(out_ref.dtype)
+
+
+def acts_kernel(own_ref, up_in, down_in, far_in, gate_ref, up_ref, acts_ref, grams_ref):
     width = gate_ref.shape[0]
-    total = sums_ref[0, :width].astype(F32)
-    for peer in range(1, sums_ref.shape[0]):
-        total = total + sums_ref[peer, :width].astype(F32)
-    grad_hidden = total.astype(BF16).astype(F32)
-    gate, up = gate_ref[...], up_ref[...]
+    peers, slabs, _ = grams_ref.shape
+    total = own_ref[...] + up_in[...].astype(F32)
+    total = total + down_in[...].astype(F32) + far_in[...].astype(F32)
+    gate, up = total[:width], total[width : 2 * width]
+    grams = total[2 * width : 2 * width + slabs].astype(BF16)
+    grad_hidden = total[2 * width + slabs :].astype(BF16).astype(F32)
     sig = jax.nn.sigmoid(gate)
     silu = gate * sig
+    gate_ref[...] = gate
+    up_ref[...] = up
     acts_ref[:width] = (grad_hidden * up * sig * (1.0 + gate * (1.0 - sig))).astype(BF16)
     acts_ref[width : 2 * width] = (grad_hidden * silu).astype(BF16)
     acts_ref[2 * width :] = (silu * up).astype(BF16)
-
-
-def step_kernel(core_ref, acts_ref, arrived_ref, grams_ref, step_ref, local_ref):
+    for peer in range(peers):
+        grams_ref[peer] = grams
+
+
+def step_kernel(place_ref, acts_ref, arrived_ref, grams_ref, step_ref, local_ref):
     peers, rows, half = grams_ref.shape
     width = acts_ref.shape[0] // 3
-    slab = (rows - width) // 2
-    core = core_ref[0]
-    kinds = ((0, 2 * width, width), (2 * width, 3 * width, width + slab))
+    slab = rows // 2
+    core = place_ref[0]
+    kinds = ((0, 2 * width, 0), (2 * width, 3 * width, slab))
     local = 0.0
     for first, end, at in kinds:
         product = 0.0
@@ -263,7 +243,7 @@
 
 
 def out_kernel(
-    core_ref, scale_ref, pt_ref, pm_ref, ht_ref, hm_ref, wd_ref, dy_ref, out_ref, ph_ref, mix_ref
+    place_ref, scale_ref, pt_ref, pm_ref, ht_ref, hm_ref, wd_ref, dy_ref, out_ref, ph_ref, mix_ref
 ):
     peers, width, half = pm_ref.shape
     part = LANES // peers
@@ -285,13 +265,13 @@
 
     acc = dot(ph_ref[...], wd_ref[...], (1, 0)) + dot(mix_ref[...], dy_ref[...], (1, 0))
     out = acc.astype(BF16)
-    theirs = pl.multiple_of((1 - core_ref[0]) * half, half)
-    mine = pl.multiple_of(core_ref[0] * half, half)
+    theirs = pl.multiple_of((1 - place_ref[0]) * half, half)
+    mine = pl.multiple_of(place_ref[0] * half, half)
     out_ref[pl.ds(theirs, half), :] = out[:half]
     out_ref[pl.ds(mine, half), :] = out[half:]
 
 
-def out_terms(core, scale, ph_theirs, ph_mine, h_theirs, h_mine, w_down, dy):
+def out_terms(place, scale, ph_theirs, ph_mine, h_theirs, h_mine, w_down, dy):
     hidden, depth = w_down.shape
     tokens = dy.shape[0]
     block = min(depth, 256)
@@ -318,47 +298,63 @@
             flops=2 * tokens * depth * hidden, bytes_accessed=2 * depth * hidden, transcendentals=0
         ),
         name="out_terms",
-    )(core, scale, ph_theirs, ph_mine, h_theirs, h_mine, w_down, dy)
+    )(place, scale, ph_theirs, ph_mine, h_theirs, h_mine, w_down, dy)
 
 
 def per_device(tokens, grad_out, w_gate, w_up, w_down, radius):
-    core = lax.axis_index(CORE).reshape(1).astype(jnp.int32)
     peers = lax.axis_size(Z)
     sources = lax.axis_size(ROW)
     rows, depth = tokens.shape
     half = sources * rows // 2
     width = w_gate.shape[1] // peers
     slab = 2 * half // peers
+    every = 3 * width + 2 * slab
+    cut = (every + 31) // 32 * 16
+    neighbour = [(z, z ^ 1) for z in range(peers)]
+    other = [(z, (z + 2 * (z % 2) - 1) % peers) for z in range(peers)]
+
+    def moved(x, by):
+        return lax.ppermute(x, Z, [(z, (z + by) % peers) for z in range(peers)])
 
     radius = jnp.broadcast_to(radius, (SUBLANES, half))
-    tokens, grad_out, core, radius = lax.optimization_barrier(
-        (tokens, grad_out, core, radius)
-    )
+    place = jnp.stack([lax.axis_index(CORE), lax.axis_index(Z)]).astype(jnp.int32)
+    tokens, grad_out, place, radius = lax.optimization_barrier((tokens, grad_out, place, radius))
     fetched = exchange(copies_in(tokens, grad_out, sources), ROW)
-    theirs, mine, dy = terms(core, fetched, w_gate, w_up, w_down, peers)
+    theirs, mine, dy = terms(place, fetched, w_gate, w_up, w_down, peers)
     arrived = swap_cores(theirs)
-    chip, chip_gh = local_kernel(
-        add_kernel,
-        [((peers, 2 * (width + slab), half), BF16), ((peers, width, half), BF16)],
-        (mine, arrived),
-    )
-    sums = exchange(chip, Z)
-    sent, gate, up = local_kernel(
-        middle_kernel,
+    first, second, keep = local_kernel(
+        split_kernel,
         [
-            ((peers, width + 2 * slab, half), BF16),
+            ((peers // 2, cut, half), BF16),
+            ((peers // 2, every - cut, half), BF16),
+            ((peers // 2, every, half), F32),
+        ],
+        (place, mine, arrived),
+    )
+    first = lax.ppermute(first, Z, neighbour)
+    second = lax.ppermute(second, Z, other)
+    block = ((every, half), BF16)
+    own, up_block, down_block, far_block = local_kernel(
+        pair_kernel, [((every, half), F32), block, block, block], (place, keep, first, second)
+    )
+    blocks = (moved(up_block, 2), moved(down_block, -2), moved(far_block, 4))
+    gate, up, acts, grams = local_kernel(
+        acts_kernel,
+        [
             ((width, half), F32),
             ((width, half), F32),
+            ((3 * width, half), BF16),
+            ((peers, 2 * slab, half), BF16),
         ],
-        (sums, chip_gh),
-    )
-    sums = exchange(sent, Z)
-    (acts,) = local_kernel(acts_kernel, [((3 * width, half), BF16)], (sums, gate, up))
+        (own, *blocks),
+    )
     arrived = swap_cores(acts)
+    arrived, grams = lax.optimization_barrier((arrived, grams))
+    sums = exchange(grams, Z)
     step, local = local_kernel(
         step_kernel,
         [((2 * width, half), F32), ((2 * sources, SUBLANES, LANES), F32)],
-        (core, acts, arrived, sums),
+        (place, acts, arrived, sums),
     )
     plane = exchange(local, (*ROW, CORE))
     (sent,) = local_kernel(
@@ -373,13 +369,13 @@
     ph_mine, h_mine = lax.optimization_barrier((ph_mine, h_mine))
     ph_theirs = swap_cores(ph_mine)
     h_theirs = swap_cores(h_mine)
-    partial_out = out_terms(core, scale, ph_theirs, ph_mine, h_theirs, h_mine, w_down, dy)
+    partial_out = out_terms(place, scale, ph_theirs, ph_mine, h_theirs, h_mine, w_down, dy)
     partial_out, norm = lax.optimization_barrier((partial_out, norm[0, :1]))
     parts = exchange(partial_out.reshape(sources, rows, depth), ROW)
     return (jnp.sum(parts.astype(F32), 0).astype(BF16), norm)
 
 
-TERMS_MIB = 60
+TERMS_MIB = 24
 
 
 def solution(mesh):

time: 173 us -> 161 us (0.931)
  blocking collectives: 137 us -> 101 us
  waiting for transfers between devices: 5.58 us -> 23.1 us
  starting transfers between devices: 7.41 us -> 18.3 us
  Pallas kernels: 18.4 us -> 13.8 us
    all_to_all x7 -> x6, blocking collectives: 137 us -> 101 us  [exchange(): return lax.all_to_all(x, axis, 0, 0, tiled=True)]
    ppermute x0 -> x5, waiting for transfers between devices: none -> 17.8 us  [the longest x3 9.98 us: moved(): return lax.ppermute(x, Z, [(z, (z + by) % peers) for z in range(peers)])]
    ppermute x0 -> x5, starting transfers between devices: none -> 13.8 us  [the longest x3 7.39 us: moved(): return lax.ppermute(x, Z, [(z, (z + by) % peers) for z in range(peers)])]
    pallas_call x1, Pallas kernels: 11.5 us -> 7.15 us  [terms(): pl.pallas_call(terms_kernel, grid=(steps + 1,), in_specs=[SMEM] + [VMEM]...]
    ppermute x4, starting transfers between devices: 7.41 us -> 4.57 us  [swap_cores(): return lax.ppermute(x, CORE, [(0, 1), (1, 0)])]
    pallas_call x1, Pallas kernels: 2.59 us -> 0.19 us  [copies_in(): pl.pallas_call(copies_in_kernel, in_specs=[pl.BlockSpec(memory_space=pl.A...]
  transfers between devices with their start and end apart: 4 -> 9, of which waited for: 3 -> 6; matrix products, arithmetic and copies ran while one was open for 0% -> 0% of each run, Pallas kernels for 0% -> 0%
where the time goes in v1:
time: 161 us
  blocking collectives  101 us (63%)
  waiting for transfers between devices  23.1 us (14%)
  starting transfers between devices  18.3 us (11%)
  Pallas kernels  13.8 us (9%)
  local copies, waits for them, and re-layouts  2.04 us (1%)
    all_to_all x6, blocking collectives, exchange(): return lax.all_to_all(x, axis, 0, 0, tiled=True)  101 us
    ppermute x3, waiting for transfers between devices, moved(): return lax.ppermute(x, Z, [(z, (z + by) % peers) for z in range(peers)])  9.98 us
    ppermute x1, waiting for transfers between devices, per_device(): second = lax.ppermute(second, Z, other)  7.78 us
    ppermute x3, starting transfers between devices, moved(): return lax.ppermute(x, Z, [(z, (z + by) % peers) for z in range(peers)])  7.39 us
    pallas_call x1, Pallas kernels, terms(): pl.pallas_call(terms_kernel, grid=(steps + 1,), in_specs=[SMEM] + [VMEM]...  7.15 us
    ppermute x4, waiting for transfers between devices, swap_cores(): return lax.ppermute(x, CORE, [(0, 1), (1, 0)])  5.37 us
    ppermute x1, starting transfers between devices, per_device(): second = lax.ppermute(second, Z, other)  4.66 us
    ppermute x4, starting transfers between devices, swap_cores(): return lax.ppermute(x, CORE, [(0, 1), (1, 0)])  4.57 us
  transfers between devices with their start and end apart: 9, of which 6 were waited for; matrix products, arithmetic and copies ran while one was open for 0% of the time, Pallas kernels for 0%

profile of v1, /device:TPU:1, one launch (start us, length us, event | category | flops | bytes accessed | tf_op | source)
XLA Modules:
  0.0 160.9 jit_solution(13687738462135097856)
XLA Ops:
  1.3 0.1 pad_add_fusion.place_ref
  1.4 0.0 copy-start.3
  1.4 0.8 copy-done.3
  2.1 0.0 copy-start.4
  2.1 0.8 copy-done.4
  2.9 0.0 copy-start
  2.9 0.0 copy-start.1
  2.9 0.0 copy-start.2
  2.9 0.2 copies_in.1
  3.1 23.7 %all_to_all.30.in_ref = bf16[16,32,1024]{2,1,0:T(8,128)(2,1)S(1)} all-to-all(bf16[16,32,1024]{2,1,0:T(8,128)(2,1)S(1)} %copies_in.1), channel_id=1, replica_groups=mesh['row_0'=4,'row_1'=4,'col_0'=8,'col_1'=2] {'row_0','row_1'}, dimensions={0} | all-to-all | bytes 2097152 | tf_op jit(solution)/shard_map/all_to_all | solution.py:29
  26.8 0.0 copy-done
  26.8 0.0 copy-done.1
  26.8 0.0 copy-done.2
  26.8 7.2 %terms.1 = (bf16[8,688,128]{2,1,0:T(8,128)(2,1)S(1)}, bf16[8,688,128]{2,1,0:T(8,128)(2,1)S(1)}, bf16[256,1024]{1,0:T(8,128)(2,1)S(1)}) custom-call(s32[2]{0:T(128)S(1)} %pad_add_fusion.place_ref, bf16[16,32,1024]{2,1,0:T(8,128)(2,1)S(1)} %all_to_all.30.in_ref, bf16[1024,1664]{1,0:T(8,128)(2,1)S(1)} %copy-done.1, bf16[1024,1664]{1,0:T(8,128)(2,1)S(1)} %copy-done.2, ...), custom_call_target="tpu_custom_call" | custom-call | flops 2617245696 | bytes 10223616 | tf_op jit(solution)/shard_map/terms/pallas_call | solution.py:141
  33.9 2.1 %collective-permute-start = (bf16[8,688,128]{2,1,0:T(8,128)(2,1)S(1)}, bf16[8,688,128]{2,1,0:T(8,128)(2,1)S(1)}, u32[]{:S(2)}, u32[]{:S(2)}) collective-permute-start(bf16[8,688,128]{2,1,0:T(8,128)(2,1)S(1)} %get-tuple-element.35), channel_id=1, source_target_pairs={{0,1},{1,0},{2,3},{3,2},{4,5},{5,4},{6,7},{7,6},{8,9},{9,8},{10,11... | collective-permute-start | bytes 4227080 | tf_op jit(solution)/shard_map/ppermute | solution.py:33
  36.1 2.8 %collective-permute-done.arrived_ref = bf16[8,688,128]{2,1,0:T(8,128)(2,1)S(1)} collective-permute-done((bf16[8,688,128]{2,1,0:T(8,128)(2,1)S(1)}, bf16[8,688,128]{2,1,0:T(8,128)(2,1)S(1)}, u32[]{:S(2)}, u32[]{:S(2)}) %collective-permute-start) | collective-permute-done | bytes 1409056 | tf_op jit(solution)/shard_map/ppermute | solution.py:33
  38.9 0.8 shard_map.80
  39.7 1.7 %collective-permute-start.1 = (bf16[4,352,128]{2,1,0:T(8,128)(2,1)S(1)}, bf16[4,352,128]{2,1,0:T(8,128)(2,1)S(1)}, u32[]{:S(2)}, u32[]{:S(2)}) collective-permute-start(bf16[4,352,128]{2,1,0:T(8,128)(2,1)S(1)} %get-tuple-element.37), channel_id=1, source_target_pairs={{0,2},{2,0},{4,6},{6,4},{8,10},{10,8},{12,14},{14,12},{1,3},{3,1},... | collective-permute-start | bytes 1081352 | tf_op jit(solution)/shard_map/ppermute | solution.py:334
  41.5 4.7 %collective-permute-start.2 = (bf16[4,336,128]{2,1,0:T(8,128)(2,1)S(1)}, bf16[4,336,128]{2,1,0:T(8,128)(2,1)S(1)}, u32[]{:S(2)}, u32[]{:S(2)}) collective-permute-start(bf16[4,336,128]{2,1,0:T(8,128)(2,1)S(1)} %get-tuple-element.38), channel_id=1, source_target_pairs={{0,14},{2,4},{4,2},{6,8},{8,6},{10,12},{12,10},{14,0},{1,15},{3,5}... | collective-permute-start | bytes 1032200 | tf_op jit(solution)/shard_map/ppermute | solution.py:335
  46.1 7.8 %collective-permute-done.2.second_ref = bf16[4,336,128]{2,1,0:T(8,128)(2,1)S(1)} collective-permute-done((bf16[4,336,128]{2,1,0:T(8,128)(2,1)S(1)}, bf16[4,336,128]{2,1,0:T(8,128)(2,1)S(1)}, u32[]{:S(2)}, u32[]{:S(2)}) %collective-permute-start.2) | collective-permute-done | bytes 344096 | tf_op jit(solution)/shard_map/ppermute | solution.py:335
  53.9 0.0 collective-permute-done.1.first_ref
  53.9 0.7 shard_map.81
  54.6 0.1 collective-permute-start.3
  54.7 3.6 %collective-permute-start.4 = (bf16[688,128]{1,0:T(8,128)(2,1)S(1)}, bf16[688,128]{1,0:T(8,128)(2,1)S(1)}, u32[]{:S(2)}, u32[]{:S(2)}) collective-permute-start(bf16[688,128]{1,0:T(8,128)(2,1)S(1)} %get-tuple-element.41), channel_id=1, source_target_pairs={{0,12},{2,14},{4,0},{6,2},{8,4},{10,6},{12,8},{14,10},{1,13},{3,15... | collective-permute-start | bytes 528392 | tf_op jit(solution)/shard_map/ppermute | solution.py:317
  58.3 3.7 %collective-permute-start.5 = (bf16[688,128]{1,0:T(8,128)(2,1)S(1)}, bf16[688,128]{1,0:T(8,128)(2,1)S(1)}, u32[]{:S(2)}, u32[]{:S(2)}) collective-permute-start(bf16[688,128]{1,0:T(8,128)(2,1)S(1)} %get-tuple-element.42), channel_id=1, source_target_pairs={{0,8},{2,10},{4,12},{6,14},{8,0},{10,2},{12,4},{14,6},{1,9},{3,11}... | collective-permute-start | bytes 528392 | tf_op jit(solution)/shard_map/ppermute | solution.py:317
  62.0 1.6 %collective-permute-done.3.up_in = bf16[688,128]{1,0:T(8,128)(2,1)S(1)} collective-permute-done((bf16[688,128]{1,0:T(8,128)(2,1)S(1)}, bf16[688,128]{1,0:T(8,128)(2,1)S(1)}, u32[]{:S(2)}, u32[]{:S(2)}) %collective-permute-start.3) | collective-permute-done | bytes 176160 | tf_op jit(solution)/shard_map/ppermute | solution.py:317
  63.6 8.4 %collective-permute-done.4.down_in = bf16[688,128]{1,0:T(8,128)(2,1)S(1)} collective-permute-done((bf16[688,128]{1,0:T(8,128)(2,1)S(1)}, bf16[688,128]{1,0:T(8,128)(2,1)S(1)}, u32[]{:S(2)}, u32[]{:S(2)}) %collective-permute-start.4) | collective-permute-done | bytes 176160 | tf_op jit(solution)/shard_map/ppermute | solution.py:317
  72.0 0.0 collective-permute-done.5.far_in
  72.0 0.1 shard_map.82
  72.1 0.9 collective-permute-start.6
  73.1 1.0 collective-permute-done.6.arrived_ref
  74.1 15.4 %all_to_all.31.grams_ref = bf16[8,64,128]{2,1,0:T(8,128)(2,1)S(1)} all-to-all(bf16[8,64,128]{2,1,0:T(8,128)(2,1)S(1)} %get-tuple-element.46), channel_id=1, replica_groups=mesh['row_0'=4,'row_1'=4,'col_0'=8,'col_1'=2] {'col_0'}, dimensions={0} | all-to-all | bytes 262144 | tf_op jit(solution)/shard_map/all_to_all | solution.py:29
  89.5 0.9 shard_map.83
  90.5 12.7 %all_to_all.32.plane_ref = f32[32,8,128]{2,1,0:T(8,128)S(1)} all-to-all(f32[32,8,128]{2,1,0:T(8,128)S(1)} %get-tuple-element.47), channel_id=1, replica_groups=mesh['row_0'=4,'row_1'=4,'col_0'=8,'col_1'=2] {'row_0','row_1','col_1'}, dimensions={0} | all-to-all | bytes 262144 | tf_op jit(solution)/shard_map/all_to_all | solution.py:29
  103.2 0.1 shard_map.84
  103.2 18.9 %all_to_all.33.ends_ref.hm_ref = bf16[8,224,128]{2,1,0:T(8,128)(2,1)S(1)} all-to-all(bf16[8,224,128]{2,1,0:T(8,128)(2,1)S(1)} %shard_map.84), channel_id=1, replica_groups=mesh['row_0'=4,'row_1'=4,'col_0'=8,'col_1'=2] {'col_0'}, dimensions={0} | all-to-all | bytes 917504 | tf_op jit(solution)/shard_map/all_to_all | solution.py:29
  122.1 0.1 shard_map.85
  122.2 17.3 %all_to_all.34.pm_ref = bf16[8,208,128]{2,1,0:T(8,128)(2,1)S(1)} all-to-all(bf16[8,208,128]{2,1,0:T(8,128)(2,1)S(1)} %get-tuple-element.53), channel_id=1, replica_groups=mesh['row_0'=4,'row_1'=4,'col_0'=8,'col_1'=2] {'col_0'}, dimensions={0} | all-to-all | bytes 851968 | tf_op jit(solution)/shard_map/all_to_all | solution.py:29
  139.5 1.5 collective-permute-start.8
  140.9 0.0 collective-permute-start.7
  140.9 0.5 slice.3
  141.5 1.5 collective-permute-done.7.pt_ref
  143.0 0.0 collective-permute-done.8.ht_ref
  143.0 3.7 %out_terms.1 = bf16[256,1024]{1,0:T(8,128)(2,1)S(1)} custom-call(s32[2]{0:T(128)S(1)} %pad_add_fusion.place_ref, f32[8,128]{1,0:T(8,128)S(1)} %get-tuple-element.52.scale_ref, bf16[8,208,128]{2,1,0:T(8,128)(2,1)S(1)} %collective-permute-done.7.pt_ref, bf16[8,208,128]{2,1,0:T(8,128)(2,1)S(1)} %all_to_all.34.pm_ref, ...), custom_call_target="tpu_custom_call" | custom-call | flops 872415232 | bytes 3407872 | tf_op jit(solution)/shard_map/out_terms/pallas_call | solution.py:280
  146.7 13.5 %all_to_all.35 = bf16[16,16,1024]{2,1,0:T(8,128)(2,1)S(1)} all-to-all(bf16[16,16,1024]{2,1,0:T(8,128)(2,1)S(1)} %bitcast.6), channel_id=1, replica_groups=mesh['row_0'=4,'row_1'=4,'col_0'=8,'col_1'=2] {'row_0','row_1'}, dimensions={0} | all-to-all | bytes 1048576 | tf_op jit(solution)/shard_map/all_to_all | solution.py:29
  160.2 0.7 reduce_sum.12
  (1 shorter events, 0.0 us)
Async XLA Ops:
  1.4 0.8 copy-start.3
  2.1 0.8 copy-start.4
  2.9 23.9 %copy-start = (bf16[1664,1024]{1,0:T(8,128)(2,1)S(1)}, bf16[1664,1024]{1,0:T(8,128)(2,1)}, u32[]{:S(2)}) copy-start(bf16[1664,1024]{1,0:T(8,128)(2,1)} %wd_ref.3) | copy-start | bytes 10223620
  2.9 23.9 %copy-start.1 = (bf16[1024,1664]{1,0:T(8,128)(2,1)S(1)}, bf16[1024,1664]{1,0:T(8,128)(2,1)}, u32[]{:S(2)}) copy-start(bf16[1024,1664]{1,0:T(8,128)(2,1)} %wg_ref.1) | copy-start | bytes 10223620
  2.9 23.9 %copy-start.2 = (bf16[1024,1664]{1,0:T(8,128)(2,1)S(1)}, bf16[1024,1664]{1,0:T(8,128)(2,1)}, u32[]{:S(2)}) copy-start(bf16[1024,1664]{1,0:T(8,128)(2,1)} %wu_ref.1) | copy-start | bytes 10223620
  33.9 5.0 %collective-permute-start = (bf16[8,688,128]{2,1,0:T(8,128)(2,1)S(1)}, bf16[8,688,128]{2,1,0:T(8,128)(2,1)S(1)}, u32[]{:S(2)}, u32[]{:S(2)}) collective-permute-start(bf16[8,688,128]{2,1,0:T(8,128)(2,1)S(1)} %get-tuple-element.35), channel_id=1, source_target_pairs={{0,1},{1,0},{2,3},{3,2},{4,5},{5,4},{6,7},{7,6},{8,9},{9,8},{10,11... | collective-permute-start | bytes 4227080 | tf_op jit(solution)/shard_map/ppermute | solution.py:33
  39.7 14.2 %collective-permute-start.1 = (bf16[4,352,128]{2,1,0:T(8,128)(2,1)S(1)}, bf16[4,352,128]{2,1,0:T(8,128)(2,1)S(1)}, u32[]{:S(2)}, u32[]{:S(2)}) collective-permute-start(bf16[4,352,128]{2,1,0:T(8,128)(2,1)S(1)} %get-tuple-element.37), channel_id=1, source_target_pairs={{0,2},{2,0},{4,6},{6,4},{8,10},{10,8},{12,14},{14,12},{1,3},{3,1},... | collective-permute-start | bytes 1081352 | tf_op jit(solution)/shard_map/ppermute | solution.py:334
  41.5 12.4 %collective-permute-start.2 = (bf16[4,336,128]{2,1,0:T(8,128)(2,1)S(1)}, bf16[4,336,128]{2,1,0:T(8,128)(2,1)S(1)}, u32[]{:S(2)}, u32[]{:S(2)}) collective-permute-start(bf16[4,336,128]{2,1,0:T(8,128)(2,1)S(1)} %get-tuple-element.38), channel_id=1, source_target_pairs={{0,14},{2,4},{4,2},{6,8},{8,6},{10,12},{12,10},{14,0},{1,15},{3,5}... | collective-permute-start | bytes 1032200 | tf_op jit(solution)/shard_map/ppermute | solution.py:335
  54.6 9.0 %collective-permute-start.3 = (bf16[688,128]{1,0:T(8,128)(2,1)S(1)}, bf16[688,128]{1,0:T(8,128)(2,1)S(1)}, u32[]{:S(2)}, u32[]{:S(2)}) collective-permute-start(bf16[688,128]{1,0:T(8,128)(2,1)S(1)} %get-tuple-element.40), channel_id=1, source_target_pairs={{0,4},{2,6},{4,8},{6,10},{8,12},{10,14},{12,0},{14,2},{1,5},{3,7},... | collective-permute-start | bytes 528392 | tf_op jit(solution)/shard_map/ppermute | solution.py:317
  54.7 17.3 %collective-permute-start.4 = (bf16[688,128]{1,0:T(8,128)(2,1)S(1)}, bf16[688,128]{1,0:T(8,128)(2,1)S(1)}, u32[]{:S(2)}, u32[]{:S(2)}) collective-permute-start(bf16[688,128]{1,0:T(8,128)(2,1)S(1)} %get-tuple-element.41), channel_id=1, source_target_pairs={{0,12},{2,14},{4,0},{6,2},{8,4},{10,6},{12,8},{14,10},{1,13},{3,15... | collective-permute-start | bytes 528392 | tf_op jit(solution)/shard_map/ppermute | solution.py:317
  58.3 13.7 %collective-permute-start.5 = (bf16[688,128]{1,0:T(8,128)(2,1)S(1)}, bf16[688,128]{1,0:T(8,128)(2,1)S(1)}, u32[]{:S(2)}, u32[]{:S(2)}) collective-permute-start(bf16[688,128]{1,0:T(8,128)(2,1)S(1)} %get-tuple-element.42), channel_id=1, source_target_pairs={{0,8},{2,10},{4,12},{6,14},{8,0},{10,2},{12,4},{14,6},{1,9},{3,11}... | collective-permute-start | bytes 528392 | tf_op jit(solution)/shard_map/ppermute | solution.py:317
  72.1 2.0 %collective-permute-start.6 = (bf16[624,128]{1,0:T(8,128)(2,1)S(1)}, bf16[624,128]{1,0:T(8,128)(2,1)S(1)}, u32[]{:S(2)}, u32[]{:S(2)}) collective-permute-start(bf16[624,128]{1,0:T(8,128)(2,1)S(1)} %get-tuple-element.43.acts_ref), channel_id=1, source_target_pairs={{0,1},{1,0},{2,3},{3,2},{4,5},{5,4},{6,7},{7,6},{8,9},{9,8},{10,11... | collective-permute-start | bytes 479240 | tf_op jit(solution)/shard_map/ppermute | solution.py:33
  139.5 3.5 %collective-permute-start.8 = (bf16[8,224,128]{2,1,0:T(8,128)(2,1)S(1)}, bf16[8,224,128]{2,1,0:T(8,128)(2,1)S(1)}, u32[]{:S(2)}, u32[]{:S(2)}) collective-permute-start(bf16[8,224,128]{2,1,0:T(8,128)(2,1)S(1)} %all_to_all.33.ends_ref.hm_ref), channel_id=1, source_target_pairs={{0,1},{1,0},{2,3},{3,2},{4,5},{5,4},{6,7},{7,6},{8,9},{9,8},{10,11... | collective-permute-start | bytes 1376264 | tf_op jit(solution)/shard_map/ppermute | solution.py:33
  140.9 2.1 %collective-permute-start.7 = (bf16[8,208,128]{2,1,0:T(8,128)(2,1)S(1)}, bf16[8,208,128]{2,1,0:T(8,128)(2,1)S(1)}, u32[]{:S(2)}, u32[]{:S(2)}) collective-permute-start(bf16[8,208,128]{2,1,0:T(8,128)(2,1)S(1)} %all_to_all.34.pm_ref), channel_id=1, source_target_pairs={{0,1},{1,0},{2,3},{3,2},{4,5},{5,4},{6,7},{7,6},{8,9},{9,8},{10,11... | collective-permute-start | bytes 1277960 | tf_op jit(solution)/shard_map/ppermute | solution.py:33

commit v2 on v1

--- a/solution.py
+++ b/solution.py
@@ -85,7 +85,6 @@
     rows = rows2 // 2
     tokens = sources * rows
     half = tokens // 2
-    slab = tokens // peers
     part = LANES // peers
     width = steps * part
     core = place_ref[0]
@@ -93,15 +92,6 @@
 
     @pl.when(j == 0)
     def _():
-        for kind in range(2):
-            row_at = 2 * width + kind * slab
-            a = in_ref[:, kind * rows : (kind + 1) * rows, :].reshape(tokens, depth)
-            for side, out_ref in sides:
-                own = in_ref[
-                    pl.ds(side * (sources // 2), sources // 2), kind * rows : (kind + 1) * rows, :
-                ].reshape(half, depth)
-                gram = dot(a, own, (1, 1)).astype(BF16)
-                out_ref[:, row_at : row_at + slab, :] = gram.reshape(peers, slab, half)
         for at, side in ((0, 1 - core), (half, core)):
             own = in_ref[pl.ds(side * (sources // 2), sources // 2), rows:, :]
             ord_ref[at : at + half] = own.reshape(half, depth)
@@ -126,7 +116,7 @@
             for step in range(first, end):
                 piece = block[(step - first) * LANES : (step - first + 1) * LANES]
                 piece = piece.reshape(peers, part, tokens)
-                to = 2 * width + 2 * slab + step * part
+                to = 2 * width + step * part
                 theirs_ref[:, to : to + part, :] = piece[:, :, :half]
                 mine_ref[:, to : to + part, :] = piece[:, :, half:]
 
@@ -135,7 +125,7 @@
     depth, hidden = w_gate.shape
     tokens = fetched.shape[0] * fetched.shape[1] // 2
     steps = hidden // LANES
-    rows = 3 * hidden // peers + 2 * tokens // peers
+    rows = 3 * hidden // peers
     out = jax.ShapeDtypeStruct((peers, rows, tokens // 2), BF16)
     dy = jax.ShapeDtypeStruct((tokens, depth), BF16)
     return pl.pallas_call(
@@ -153,6 +143,39 @@
     )(place, fetched, w_gate, w_up, w_down)
 
 
+def gram_kernel(place_ref, in_ref, theirs_ref, mine_ref):
+    sources, rows2, depth = in_ref.shape
+    rows = rows2 // 2
+    half = sources * rows // 2
+    core, row = place_ref[0], place_ref[2]
+    for side, out_ref in ((1 - core, theirs_ref), (core, mine_ref)):
+        for kind in range(2):
+            at = slice(kind * rows, (kind + 1) * rows)
+            every = in_ref[pl.ds(side * (sources // 2), sources // 2), at, :]
+            out_ref[at] = dot(in_ref[row, at], every.reshape(half, depth), (1, 1)).astype(BF16)
+
+
+def gram_sum_kernel(*refs):
+    *terms_in, out_ref = refs
+    total = terms_in[0][...].astype(F32)
+    for ref in terms_in[1:]:
+        total = total + ref[...].astype(F32)
+    total = total.astype(BF16)
+    if len(out_ref.shape) == 2:
+        out_ref[...] = total
+    else:
+        for peer in range(out_ref.shape[0]):
+            out_ref[peer] = total
+
+
+def gram_table_kernel(parts_ref, table_ref):
+    sources, rows2, half = parts_ref.shape
+    rows = rows2 // 2
+    for kind in range(2):
+        part = parts_ref[:, kind * rows : (kind + 1) * rows, :]
+        table_ref[kind] = part.reshape(sources * rows, half)
+
+
 def split_kernel(place_ref, mine_ref, arrived_ref, first_ref, second_ref, keep_ref):
     parity = lax.rem(place_ref[1], 2)
     cut = first_ref.shape[1]
@@ -174,14 +197,12 @@
         out_ref[cut:] = (keep_ref[q, cut:] + second_ref[q].astype(F32)).astype(out_ref.dtype)
 
 
-def acts_kernel(own_ref, up_in, down_in, far_in, gate_ref, up_ref, acts_ref, grams_ref):
+def acts_kernel(own_ref, up_in, down_in, far_in, gate_ref, up_ref, acts_ref):
     width = gate_ref.shape[0]
-    peers, slabs, _ = grams_ref.shape
     total = own_ref[...] + up_in[...].astype(F32)
     total = total + down_in[...].astype(F32) + far_in[...].astype(F32)
     gate, up = total[:width], total[width : 2 * width]
-    grams = total[2 * width : 2 * width + slabs].astype(BF16)
-    grad_hidden = total[2 * width + slabs :].astype(BF16).astype(F32)
+    grad_hidden = total[2 * width :].astype(BF16).astype(F32)
     sig = jax.nn.sigmoid(gate)
     silu = gate * sig
     gate_ref[...] = gate
@@ -189,22 +210,19 @@
     acts_ref[:width] = (grad_hidden * up * sig * (1.0 + gate * (1.0 - sig))).astype(BF16)
     acts_ref[width : 2 * width] = (grad_hidden * silu).astype(BF16)
     acts_ref[2 * width :] = (silu * up).astype(BF16)
-    for peer in range(peers):
-        grams_ref[peer] = grams
 
 
 def step_kernel(place_ref, acts_ref, arrived_ref, grams_ref, step_ref, local_ref):
-    peers, rows, half = grams_ref.shape
+    half = grams_ref.shape[2]
     width = acts_ref.shape[0] // 3
-    slab = rows // 2
     core = place_ref[0]
-    kinds = ((0, 2 * width, 0), (2 * width, 3 * width, slab))
+    kinds = ((0, 2 * width, 0), (2 * width, 3 * width, 1))
     local = 0.0
-    for first, end, at in kinds:
+    for first, end, kind in kinds:
         product = 0.0
         for side, part_ref in ((1 - core, arrived_ref), (core, acts_ref)):
-            gram = grams_ref[pl.ds(side * (peers // 2), peers // 2), at : at + slab, :]
-            product += dot(part_ref[first:end], gram.reshape(half, half), (1, 0))
+            gram = grams_ref[kind, pl.ds(pl.multiple_of(side * half, half), half), :]
+            product += dot(part_ref[first:end], gram, (1, 0))
         local += jnp.sum(acts_ref[first:end].astype(F32) * product)
         if first == 0:
             step_ref[...] = product
@@ -307,8 +325,7 @@
     rows, depth = tokens.shape
     half = sources * rows // 2
     width = w_gate.shape[1] // peers
-    slab = 2 * half // peers
-    every = 3 * width + 2 * slab
+    every = 3 * width
     cut = (every + 31) // 32 * 16
     neighbour = [(z, z ^ 1) for z in range(peers)]
     other = [(z, (z + 2 * (z % 2) - 1) % peers) for z in range(peers)]
@@ -317,11 +334,19 @@
         return lax.ppermute(x, Z, [(z, (z + by) % peers) for z in range(peers)])
 
     radius = jnp.broadcast_to(radius, (SUBLANES, half))
-    place = jnp.stack([lax.axis_index(CORE), lax.axis_index(Z)]).astype(jnp.int32)
+    place = jnp.stack([lax.axis_index(axis) for axis in (CORE, Z, ROW)]).astype(jnp.int32)
     tokens, grad_out, place, radius = lax.optimization_barrier((tokens, grad_out, place, radius))
     fetched = exchange(copies_in(tokens, grad_out, sources), ROW)
-    theirs, mine, dy = terms(place, fetched, w_gate, w_up, w_down, peers)
-    arrived = swap_cores(theirs)
+    flat = ((2 * rows, half), BF16)
+    theirs, gram = local_kernel(gram_kernel, [flat, flat], (place, fetched))
+    fetched, theirs = lax.optimization_barrier((fetched, theirs))
+    theirs = swap_cores(theirs)
+    theirs_wide, mine, dy = terms(place, fetched, w_gate, w_up, w_down, peers)
+    (gram,) = local_kernel(gram_sum_kernel, [flat], (gram, theirs))
+    theirs_wide, gram = lax.optimization_barrier((theirs_wide, gram))
+    arrived = swap_cores(theirs_wide)
+    theirs = lax.ppermute(gram, Z, neighbour)
+    (gram,) = local_kernel(gram_sum_kernel, [flat], (gram, theirs))
     first, second, keep = local_kernel(
         split_kernel,
         [
@@ -333,24 +358,25 @@
     )
     first = lax.ppermute(first, Z, neighbour)
     second = lax.ppermute(second, Z, other)
+    others = (moved(gram, 2), moved(gram, -2), moved(gram, 4))
+    (grams,) = local_kernel(gram_sum_kernel, [((sources, 2 * rows, half), BF16)], (gram, *others))
     block = ((every, half), BF16)
     own, up_block, down_block, far_block = local_kernel(
         pair_kernel, [((every, half), F32), block, block, block], (place, keep, first, second)
     )
     blocks = (moved(up_block, 2), moved(down_block, -2), moved(far_block, 4))
-    gate, up, acts, grams = local_kernel(
+    grams = exchange(grams, ROW)
+    (sums,) = local_kernel(gram_table_kernel, [((2, 2 * half, half), BF16)], (grams,))
+    gate, up, acts = local_kernel(
         acts_kernel,
         [
             ((width, half), F32),
             ((width, half), F32),
             ((3 * width, half), BF16),
-            ((peers, 2 * slab, half), BF16),
         ],
         (own, *blocks),
     )
     arrived = swap_cores(acts)
-    arrived, grams = lax.optimization_barrier((arrived, grams))
-    sums = exchange(grams, Z)
     step, local = local_kernel(
         step_kernel,
         [((2 * width, half), F32), ((2 * sources, SUBLANES, LANES), F32)],

time: 161 us -> 172 us (1.068)
  starting transfers between devices: 18.3 us -> 31.3 us
  blocking collectives: 101 us -> 96.6 us
  waiting for transfers between devices: 23.1 us -> 25.2 us
    ppermute x3 -> x6, starting transfers between devices: 7.39 us -> 13.8 us  [moved(): return lax.ppermute(x, Z, [(z, (z + by) % peers) for z in range(peers)])]
    all_to_all x6, blocking collectives: 101 us -> 96.6 us  [exchange(): return lax.all_to_all(x, axis, 0, 0, tiled=True)]
    ppermute x0 -> x1, starting transfers between devices: none -> 4.67 us  [per_device(): theirs = lax.ppermute(gram, Z, neighbour)]
    ppermute x3 -> x6, waiting for transfers between devices: 9.98 us -> 12.4 us  [moved(): return lax.ppermute(x, Z, [(z, (z + by) % peers) for z in range(peers)])]
    ppermute x4 -> x5, starting transfers between devices: 4.57 us -> 6.48 us  [swap_cores(): return lax.ppermute(x, CORE, [(0, 1), (1, 0)])]
    pallas_call x6 -> x11, Pallas kernels: 2.75 us -> 3.65 us  [local_kernel(): pl.pallas_call(body, in_specs=[SMEM if a.dtype == jnp.int32 else VMEM for...]
    ppermute x4 -> x5, waiting for transfers between devices: 5.37 us -> 4.51 us  [swap_cores(): return lax.ppermute(x, CORE, [(0, 1), (1, 0)])]
  transfers between devices with their start and end apart: 9 -> 14, of which waited for: 6 -> 7; matrix products, arithmetic and copies ran while one was open for 0% -> 0% of each run, Pallas kernels for 0% -> 4%
where the time goes in v2:
time: 172 us; the launch traced here: 171 us
  blocking collectives  96.6 us (56%)
  starting transfers between devices  31.3 us (18%)
  waiting for transfers between devices  25.2 us (15%)
  Pallas kernels  14 us (8%)
  local copies, waits for them, and re-layouts  2.04 us (1%)
    all_to_all x6, blocking collectives, exchange(): return lax.all_to_all(x, axis, 0, 0, tiled=True)  96.6 us
    ppermute x6, starting transfers between devices, moved(): return lax.ppermute(x, Z, [(z, (z + by) % peers) for z in range(peers)])  13.8 us
    ppermute x6, waiting for transfers between devices, moved(): return lax.ppermute(x, Z, [(z, (z + by) % peers) for z in range(peers)])  12.4 us
    ppermute x1, waiting for transfers between devices, per_device(): second = lax.ppermute(second, Z, other)  7.32 us
    ppermute x5, starting transfers between devices, swap_cores(): return lax.ppermute(x, CORE, [(0, 1), (1, 0)])  6.48 us
    pallas_call x1, Pallas kernels, terms(): pl.pallas_call(terms_kernel, grid=(steps + 1,), in_specs=[SMEM] + [VMEM]...  6.47 us
    ppermute x1, starting transfers between devices, per_device(): theirs = lax.ppermute(gram, Z, neighbour)  4.67 us
    ppermute x1, starting transfers between devices, per_device(): second = lax.ppermute(second, Z, other)  4.66 us
  transfers between devices with their start and end apart: 14, of which 7 were waited for; matrix products, arithmetic and copies ran while one was open for 0% of the time, Pallas kernels for 4%

profile of v2, /device:TPU:1, one launch (start us, length us, event | category | flops | bytes accessed | tf_op | source)
XLA Modules:
  0.0 171.3 jit_solution(16587254650401537902)
XLA Ops:
  1.3 0.1 pad_add_fusion.place_ref
  1.4 0.0 copy-start.3
  1.4 0.8 copy-done.3
  2.1 0.0 copy-start.4
  2.1 0.8 copy-done.4
  2.9 0.0 copy-start
  2.9 0.0 copy-start.1
  2.9 0.0 copy-start.2
  2.9 0.2 copies_in.1
  3.1 23.7 %all_to_all.30.in_ref = bf16[16,32,1024]{2,1,0:T(8,128)(2,1)S(1)} all-to-all(bf16[16,32,1024]{2,1,0:T(8,128)(2,1)S(1)} %copies_in.1), channel_id=1, replica_groups=mesh['row_0'=4,'row_1'=4,'col_0'=8,'col_1'=2] {'row_0','row_1'}, dimensions={0} | all-to-all | bytes 2097152 | tf_op jit(solution)/shard_map/all_to_all | solution.py:29
  26.8 0.9 shard_map.80
  27.7 2.1 %collective-permute-start = (bf16[32,128]{1,0:T(8,128)(2,1)S(1)}, bf16[32,128]{1,0:T(8,128)(2,1)S(1)}, u32[]{:S(2)}, u32[]{:S(2)}) collective-permute-start(bf16[32,128]{1,0:T(8,128)(2,1)S(1)} %get-tuple-element.42), channel_id=1, source_target_pairs={{0,1},{1,0},{2,3},{3,2},{4,5},{5,4},{6,7},{7,6},{8,9},{9,8},{10,11... | collective-permute-start | bytes 24584 | tf_op jit(solution)/shard_map/ppermute | solution.py:33
  29.8 0.0 copy-done
  29.8 0.0 copy-done.1
  29.8 0.0 copy-done.2
  29.8 6.5 %terms.1 = (bf16[8,624,128]{2,1,0:T(8,128)(2,1)S(1)}, bf16[8,624,128]{2,1,0:T(8,128)(2,1)S(1)}, bf16[256,1024]{1,0:T(8,128)(2,1)S(1)}) custom-call(s32[3]{0:T(128)S(1)} %pad_add_fusion.place_ref, bf16[16,32,1024]{2,1,0:T(8,128)(2,1)S(1)} %all_to_all.30.in_ref, bf16[1024,1664]{1,0:T(8,128)(2,1)S(1)} %copy-done.1, bf16[1024,1664]{1,0:T(8,128)(2,1)S(1)} %copy-done.2, ...), custom_call_target="tpu_custom_call" | custom-call | flops 2617245696 | bytes 10223616 | tf_op jit(solution)/shard_map/terms/pallas_call | solution.py:131
  36.3 0.0 collective-permute-done.refs_1_
  36.3 0.1 collective-permute-start.1
  36.4 3.0 %collective-permute-done.1.arrived_ref = bf16[8,624,128]{2,1,0:T(8,128)(2,1)S(1)} collective-permute-done((bf16[8,624,128]{2,1,0:T(8,128)(2,1)S(1)}, bf16[8,624,128]{2,1,0:T(8,128)(2,1)S(1)}, u32[]{:S(2)}, u32[]{:S(2)}) %collective-permute-start.1) | collective-permute-done | bytes 1277984 | tf_op jit(solution)/shard_map/ppermute | solution.py:33
  39.4 0.8 shard_map.82
  40.2 1.7 %collective-permute-start.2 = (bf16[4,320,128]{2,1,0:T(8,128)(2,1)S(1)}, bf16[4,320,128]{2,1,0:T(8,128)(2,1)S(1)}, u32[]{:S(2)}, u32[]{:S(2)}) collective-permute-start(bf16[4,320,128]{2,1,0:T(8,128)(2,1)S(1)} %get-tuple-element.45), channel_id=1, source_target_pairs={{0,2},{2,0},{4,6},{6,4},{8,10},{10,8},{12,14},{14,12},{1,3},{3,1},... | collective-permute-start | bytes 983048 | tf_op jit(solution)/shard_map/ppermute | solution.py:359
  41.9 4.7 %collective-permute-start.3 = (bf16[4,304,128]{2,1,0:T(8,128)(2,1)S(1)}, bf16[4,304,128]{2,1,0:T(8,128)(2,1)S(1)}, u32[]{:S(2)}, u32[]{:S(2)}) collective-permute-start(bf16[4,304,128]{2,1,0:T(8,128)(2,1)S(1)} %get-tuple-element.46), channel_id=1, source_target_pairs={{0,14},{2,4},{4,2},{6,8},{8,6},{10,12},{12,10},{14,0},{1,15},{3,5}... | collective-permute-start | bytes 933896 | tf_op jit(solution)/shard_map/ppermute | solution.py:360
  46.6 7.3 %collective-permute-done.3.second_ref = bf16[4,304,128]{2,1,0:T(8,128)(2,1)S(1)} collective-permute-done((bf16[4,304,128]{2,1,0:T(8,128)(2,1)S(1)}, bf16[4,304,128]{2,1,0:T(8,128)(2,1)S(1)}, u32[]{:S(2)}, u32[]{:S(2)}) %collective-permute-start.3) | collective-permute-done | bytes 311328 | tf_op jit(solution)/shard_map/ppermute | solution.py:360
  53.9 0.0 collective-permute-done.2.first_ref
  53.9 0.7 shard_map.83
  54.6 0.1 collective-permute-start.4
  54.7 3.6 %collective-permute-start.5 = (bf16[624,128]{1,0:T(8,128)(2,1)S(1)}, bf16[624,128]{1,0:T(8,128)(2,1)S(1)}, u32[]{:S(2)}, u32[]{:S(2)}) collective-permute-start(bf16[624,128]{1,0:T(8,128)(2,1)S(1)} %get-tuple-element.49), channel_id=1, source_target_pairs={{0,12},{2,14},{4,0},{6,2},{8,4},{10,6},{12,8},{14,10},{1,13},{3,15... | collective-permute-start | bytes 479240 | tf_op jit(solution)/shard_map/ppermute | solution.py:334
  58.2 3.7 %collective-permute-start.6 = (bf16[624,128]{1,0:T(8,128)(2,1)S(1)}, bf16[624,128]{1,0:T(8,128)(2,1)S(1)}, u32[]{:S(2)}, u32[]{:S(2)}) collective-permute-start(bf16[624,128]{1,0:T(8,128)(2,1)S(1)} %get-tuple-element.50), channel_id=1, source_target_pairs={{0,8},{2,10},{4,12},{6,14},{8,0},{10,2},{12,4},{14,6},{1,9},{3,11}... | collective-permute-start | bytes 479240 | tf_op jit(solution)/shard_map/ppermute | solution.py:334
  62.0 1.4 collective-permute-done.4.up_in
  63.4 7.3 %collective-permute-done.5.down_in = bf16[624,128]{1,0:T(8,128)(2,1)S(1)} collective-permute-done((bf16[624,128]{1,0:T(8,128)(2,1)S(1)}, bf16[624,128]{1,0:T(8,128)(2,1)S(1)}, u32[]{:S(2)}, u32[]{:S(2)}) %collective-permute-start.5) | collective-permute-done | bytes 159776 | tf_op jit(solution)/shard_map/ppermute | solution.py:334
  70.7 0.0 collective-permute-done.6.far_in
  70.8 0.1 shard_map.84
  70.9 0.9 collective-permute-start.7
  71.8 4.7 %collective-permute-start.8 = (bf16[32,128]{1,0:T(8,128)(2,1)S(1)}, bf16[32,128]{1,0:T(8,128)(2,1)S(1)}, u32[]{:S(2)}, u32[]{:S(2)}) collective-permute-start(bf16[32,128]{1,0:T(8,128)(2,1)S(1)} %shard_map.81.refs_0_), channel_id=1, source_target_pairs={{0,2},{2,0},{4,6},{6,4},{8,10},{10,8},{12,14},{14,12},{1,3},{3,1},... | collective-permute-start | bytes 24584 | tf_op jit(solution)/shard_map/ppermute | solution.py:348
  76.5 1.0 collective-permute-done.8.refs_1_
  77.5 2.8 %collective-permute-start.9 = (bf16[32,128]{1,0:T(8,128)(2,1)S(1)}, bf16[32,128]{1,0:T(8,128)(2,1)S(1)}, u32[]{:S(2)}, u32[]{:S(2)}) collective-permute-start(bf16[32,128]{1,0:T(8,128)(2,1)S(1)} %shard_map.85.refs_0_), channel_id=1, source_target_pairs={{0,4},{2,6},{4,8},{6,10},{8,12},{10,14},{12,0},{14,2},{1,5},{3,7},... | collective-permute-start | bytes 24584 | tf_op jit(solution)/shard_map/ppermute | solution.py:334
  80.3 0.8 collective-permute-start.10
  81.1 2.8 %collective-permute-start.11 = (bf16[32,128]{1,0:T(8,128)(2,1)S(1)}, bf16[32,128]{1,0:T(8,128)(2,1)S(1)}, u32[]{:S(2)}, u32[]{:S(2)}) collective-permute-start(bf16[32,128]{1,0:T(8,128)(2,1)S(1)} %shard_map.85.refs_0_), channel_id=1, source_target_pairs={{0,8},{2,10},{4,12},{6,14},{8,0},{10,2},{12,4},{14,6},{1,9},{3,11}... | collective-permute-start | bytes 24584 | tf_op jit(solution)/shard_map/ppermute | solution.py:334
  83.9 0.0 collective-permute-done.9.refs_1_
  83.9 0.0 collective-permute-done.10.refs_2_
  83.9 3.6 %collective-permute-done.11.refs_3_ = bf16[32,128]{1,0:T(8,128)(2,1)S(1)} collective-permute-done((bf16[32,128]{1,0:T(8,128)(2,1)S(1)}, bf16[32,128]{1,0:T(8,128)(2,1)S(1)}, u32[]{:S(2)}, u32[]{:S(2)}) %collective-permute-start.11) | collective-permute-done | bytes 8224 | tf_op jit(solution)/shard_map/ppermute | solution.py:334
  87.5 9.5 %all_to_all.31.parts_ref = bf16[16,32,128]{2,1,0:T(8,128)(2,1)S(1)} all-to-all(bf16[16,32,128]{2,1,0:T(8,128)(2,1)S(1)} %shard_map.86), channel_id=1, replica_groups=mesh['row_0'=4,'row_1'=4,'col_0'=8,'col_1'=2] {'row_0','row_1'}, dimensions={0} | all-to-all | bytes 262144 | tf_op jit(solution)/shard_map/all_to_all | solution.py:29
  97.0 0.0 collective-permute-done.7.arrived_ref
  97.0 0.9 shard_map.88
  98.0 14.8 %all_to_all.32.plane_ref = f32[32,8,128]{2,1,0:T(8,128)S(1)} all-to-all(f32[32,8,128]{2,1,0:T(8,128)S(1)} %get-tuple-element.53), channel_id=1, replica_groups=mesh['row_0'=4,'row_1'=4,'col_0'=8,'col_1'=2] {'row_0','row_1','col_1'}, dimensions={0} | all-to-all | bytes 262144 | tf_op jit(solution)/shard_map/all_to_all | solution.py:29
  112.8 0.1 shard_map.89
  112.9 19.6 %all_to_all.33.ends_ref.hm_ref = bf16[8,224,128]{2,1,0:T(8,128)(2,1)S(1)} all-to-all(bf16[8,224,128]{2,1,0:T(8,128)(2,1)S(1)} %shard_map.89), channel_id=1, replica_groups=mesh['row_0'=4,'row_1'=4,'col_0'=8,'col_1'=2] {'col_0'}, dimensions={0} | all-to-all | bytes 917504 | tf_op jit(solution)/shard_map/all_to_all | solution.py:29
  132.5 0.1 shard_map.90
  132.6 15.3 %all_to_all.34.pm_ref = bf16[8,208,128]{2,1,0:T(8,128)(2,1)S(1)} all-to-all(bf16[8,208,128]{2,1,0:T(8,128)(2,1)S(1)} %get-tuple-element.59), channel_id=1, replica_groups=mesh['row_0'=4,'row_1'=4,'col_0'=8,'col_1'=2] {'col_0'}, dimensions={0} | all-to-all | bytes 851968 | tf_op jit(solution)/shard_map/all_to_all | solution.py:29
  147.9 3.4 %collective-permute-start.13 = (bf16[8,224,128]{2,1,0:T(8,128)(2,1)S(1)}, bf16[8,224,128]{2,1,0:T(8,128)(2,1)S(1)}, u32[]{:S(2)}, u32[]{:S(2)}) collective-permute-start(bf16[8,224,128]{2,1,0:T(8,128)(2,1)S(1)} %all_to_all.33.ends_ref.hm_ref), channel_id=1, source_target_pairs={{0,1},{1,0},{2,3},{3,2},{4,5},{5,4},{6,7},{7,6},{8,9},{9,8},{10,11... | collective-permute-start | bytes 1376264 | tf_op jit(solution)/shard_map/ppermute | solution.py:33
  151.3 0.0 collective-permute-start.12
  151.3 0.5 slice.3
  151.8 1.5 collective-permute-done.12.pt_ref
  153.4 0.0 collective-permute-done.13.ht_ref
  153.4 3.7 %out_terms.1 = bf16[256,1024]{1,0:T(8,128)(2,1)S(1)} custom-call(s32[3]{0:T(128)S(1)} %pad_add_fusion.place_ref, f32[8,128]{1,0:T(8,128)S(1)} %get-tuple-element.58.scale_ref, bf16[8,208,128]{2,1,0:T(8,128)(2,1)S(1)} %collective-permute-done.12.pt_ref, bf16[8,208,128]{2,1,0:T(8,128)(2,1)S(1)} %all_to_all.34.pm_ref, ...), custom_call_target="tpu_custom_call" | custom-call | flops 872415232 | bytes 3407872 | tf_op jit(solution)/shard_map/out_terms/pallas_call | solution.py:298
  157.0 13.6 %all_to_all.35 = bf16[16,16,1024]{2,1,0:T(8,128)(2,1)S(1)} all-to-all(bf16[16,16,1024]{2,1,0:T(8,128)(2,1)S(1)} %bitcast.7), channel_id=1, replica_groups=mesh['row_0'=4,'row_1'=4,'col_0'=8,'col_1'=2] {'row_0','row_1'}, dimensions={0} | all-to-all | bytes 1048576 | tf_op jit(solution)/shard_map/all_to_all | solution.py:29
  170.6 0.7 reduce_sum.12
  (5 shorter events, 0.0 us)
Async XLA Ops:
  1.4 0.8 copy-start.3
  2.1 0.8 copy-start.4
  2.9 26.9 %copy-start = (bf16[1664,1024]{1,0:T(8,128)(2,1)S(1)}, bf16[1664,1024]{1,0:T(8,128)(2,1)}, u32[]{:S(2)}) copy-start(bf16[1664,1024]{1,0:T(8,128)(2,1)} %wd_ref.3) | copy-start | bytes 10223620
  2.9 26.9 %copy-start.1 = (bf16[1024,1664]{1,0:T(8,128)(2,1)S(1)}, bf16[1024,1664]{1,0:T(8,128)(2,1)}, u32[]{:S(2)}) copy-start(bf16[1024,1664]{1,0:T(8,128)(2,1)} %wg_ref.1) | copy-start | bytes 10223620
  2.9 26.9 %copy-start.2 = (bf16[1024,1664]{1,0:T(8,128)(2,1)S(1)}, bf16[1024,1664]{1,0:T(8,128)(2,1)}, u32[]{:S(2)}) copy-start(bf16[1024,1664]{1,0:T(8,128)(2,1)} %wu_ref.1) | copy-start | bytes 10223620
  27.7 8.6 %collective-permute-start = (bf16[32,128]{1,0:T(8,128)(2,1)S(1)}, bf16[32,128]{1,0:T(8,128)(2,1)S(1)}, u32[]{:S(2)}, u32[]{:S(2)}) collective-permute-start(bf16[32,128]{1,0:T(8,128)(2,1)S(1)} %get-tuple-element.42), channel_id=1, source_target_pairs={{0,1},{1,0},{2,3},{3,2},{4,5},{5,4},{6,7},{7,6},{8,9},{9,8},{10,11... | collective-permute-start | bytes 24584 | tf_op jit(solution)/shard_map/ppermute | solution.py:33
  36.3 3.1 %collective-permute-start.1 = (bf16[8,624,128]{2,1,0:T(8,128)(2,1)S(1)}, bf16[8,624,128]{2,1,0:T(8,128)(2,1)S(1)}, u32[]{:S(2)}, u32[]{:S(2)}) collective-permute-start(bf16[8,624,128]{2,1,0:T(8,128)(2,1)S(1)} %get-tuple-element.43), channel_id=1, source_target_pairs={{0,1},{1,0},{2,3},{3,2},{4,5},{5,4},{6,7},{7,6},{8,9},{9,8},{10,11... | collective-permute-start | bytes 3833864 | tf_op jit(solution)/shard_map/ppermute | solution.py:33
  40.2 13.7 %collective-permute-start.2 = (bf16[4,320,128]{2,1,0:T(8,128)(2,1)S(1)}, bf16[4,320,128]{2,1,0:T(8,128)(2,1)S(1)}, u32[]{:S(2)}, u32[]{:S(2)}) collective-permute-start(bf16[4,320,128]{2,1,0:T(8,128)(2,1)S(1)} %get-tuple-element.45), channel_id=1, source_target_pairs={{0,2},{2,0},{4,6},{6,4},{8,10},{10,8},{12,14},{14,12},{1,3},{3,1},... | collective-permute-start | bytes 983048 | tf_op jit(solution)/shard_map/ppermute | solution.py:359
  41.9 12.0 %collective-permute-start.3 = (bf16[4,304,128]{2,1,0:T(8,128)(2,1)S(1)}, bf16[4,304,128]{2,1,0:T(8,128)(2,1)S(1)}, u32[]{:S(2)}, u32[]{:S(2)}) collective-permute-start(bf16[4,304,128]{2,1,0:T(8,128)(2,1)S(1)} %get-tuple-element.46), channel_id=1, source_target_pairs={{0,14},{2,4},{4,2},{6,8},{8,6},{10,12},{12,10},{14,0},{1,15},{3,5}... | collective-permute-start | bytes 933896 | tf_op jit(solution)/shard_map/ppermute | solution.py:360
  54.6 8.8 %collective-permute-start.4 = (bf16[624,128]{1,0:T(8,128)(2,1)S(1)}, bf16[624,128]{1,0:T(8,128)(2,1)S(1)}, u32[]{:S(2)}, u32[]{:S(2)}) collective-permute-start(bf16[624,128]{1,0:T(8,128)(2,1)S(1)} %get-tuple-element.48), channel_id=1, source_target_pairs={{0,4},{2,6},{4,8},{6,10},{8,12},{10,14},{12,0},{14,2},{1,5},{3,7},... | collective-permute-start | bytes 479240 | tf_op jit(solution)/shard_map/ppermute | solution.py:334
  54.7 16.1 %collective-permute-start.5 = (bf16[624,128]{1,0:T(8,128)(2,1)S(1)}, bf16[624,128]{1,0:T(8,128)(2,1)S(1)}, u32[]{:S(2)}, u32[]{:S(2)}) collective-permute-start(bf16[624,128]{1,0:T(8,128)(2,1)S(1)} %get-tuple-element.49), channel_id=1, source_target_pairs={{0,12},{2,14},{4,0},{6,2},{8,4},{10,6},{12,8},{14,10},{1,13},{3,15... | collective-permute-start | bytes 479240 | tf_op jit(solution)/shard_map/ppermute | solution.py:334
  58.2 12.5 %collective-permute-start.6 = (bf16[624,128]{1,0:T(8,128)(2,1)S(1)}, bf16[624,128]{1,0:T(8,128)(2,1)S(1)}, u32[]{:S(2)}, u32[]{:S(2)}) collective-permute-start(bf16[624,128]{1,0:T(8,128)(2,1)S(1)} %get-tuple-element.50), channel_id=1, source_target_pairs={{0,8},{2,10},{4,12},{6,14},{8,0},{10,2},{12,4},{14,6},{1,9},{3,11}... | collective-permute-start | bytes 479240 | tf_op jit(solution)/shard_map/ppermute | solution.py:334
  70.9 26.1 %collective-permute-start.7 = (bf16[624,128]{1,0:T(8,128)(2,1)S(1)}, bf16[624,128]{1,0:T(8,128)(2,1)S(1)}, u32[]{:S(2)}, u32[]{:S(2)}) collective-permute-start(bf16[624,128]{1,0:T(8,128)(2,1)S(1)} %get-tuple-element.51.acts_ref), channel_id=1, source_target_pairs={{0,1},{1,0},{2,3},{3,2},{4,5},{5,4},{6,7},{7,6},{8,9},{9,8},{10,11... | collective-permute-start | bytes 479240 | tf_op jit(solution)/shard_map/ppermute | solution.py:33
  71.8 5.7 %collective-permute-start.8 = (bf16[32,128]{1,0:T(8,128)(2,1)S(1)}, bf16[32,128]{1,0:T(8,128)(2,1)S(1)}, u32[]{:S(2)}, u32[]{:S(2)}) collective-permute-start(bf16[32,128]{1,0:T(8,128)(2,1)S(1)} %shard_map.81.refs_0_), channel_id=1, source_target_pairs={{0,2},{2,0},{4,6},{6,4},{8,10},{10,8},{12,14},{14,12},{1,3},{3,1},... | collective-permute-start | bytes 24584 | tf_op jit(solution)/shard_map/ppermute | solution.py:348
  77.5 6.4 %collective-permute-start.9 = (bf16[32,128]{1,0:T(8,128)(2,1)S(1)}, bf16[32,128]{1,0:T(8,128)(2,1)S(1)}, u32[]{:S(2)}, u32[]{:S(2)}) collective-permute-start(bf16[32,128]{1,0:T(8,128)(2,1)S(1)} %shard_map.85.refs_0_), channel_id=1, source_target_pairs={{0,4},{2,6},{4,8},{6,10},{8,12},{10,14},{12,0},{14,2},{1,5},{3,7},... | collective-permute-start | bytes 24584 | tf_op jit(solution)/shard_map/ppermute | solution.py:334
  80.3 3.6 %collective-permute-start.10 = (bf16[32,128]{1,0:T(8,128)(2,1)S(1)}, bf16[32,128]{1,0:T(8,128)(2,1)S(1)}, u32[]{:S(2)}, u32[]{:S(2)}) collective-permute-start(bf16[32,128]{1,0:T(8,128)(2,1)S(1)} %shard_map.85.refs_0_), channel_id=1, source_target_pairs={{0,12},{2,14},{4,0},{6,2},{8,4},{10,6},{12,8},{14,10},{1,13},{3,15... | collective-permute-start | bytes 24584 | tf_op jit(solution)/shard_map/ppermute | solution.py:334
  81.1 6.4 %collective-permute-start.11 = (bf16[32,128]{1,0:T(8,128)(2,1)S(1)}, bf16[32,128]{1,0:T(8,128)(2,1)S(1)}, u32[]{:S(2)}, u32[]{:S(2)}) collective-permute-start(bf16[32,128]{1,0:T(8,128)(2,1)S(1)} %shard_map.85.refs_0_), channel_id=1, source_target_pairs={{0,8},{2,10},{4,12},{6,14},{8,0},{10,2},{12,4},{14,6},{1,9},{3,11}... | collective-permute-start | bytes 24584 | tf_op jit(solution)/shard_map/ppermute | solution.py:334
  147.9 5.4 %collective-permute-start.13 = (bf16[8,224,128]{2,1,0:T(8,128)(2,1)S(1)}, bf16[8,224,128]{2,1,0:T(8,128)(2,1)S(1)}, u32[]{:S(2)}, u32[]{:S(2)}) collective-permute-start(bf16[8,224,128]{2,1,0:T(8,128)(2,1)S(1)} %all_to_all.33.ends_ref.hm_ref), channel_id=1, source_target_pairs={{0,1},{1,0},{2,3},{3,2},{4,5},{5,4},{6,7},{7,6},{8,9},{9,8},{10,11... | collective-permute-start | bytes 1376264 | tf_op jit(solution)/shard_map/ppermute | solution.py:33
  151.3 2.1 %collective-permute-start.12 = (bf16[8,208,128]{2,1,0:T(8,128)(2,1)S(1)}, bf16[8,208,128]{2,1,0:T(8,128)(2,1)S(1)}, u32[]{:S(2)}, u32[]{:S(2)}) collective-permute-start(bf16[8,208,128]{2,1,0:T(8,128)(2,1)S(1)} %all_to_all.34.pm_ref), channel_id=1, source_target_pairs={{0,1},{1,0},{2,3},{3,2},{4,5},{5,4},{6,7},{7,6},{8,9},{9,8},{10,11... | collective-permute-start | bytes 1277960 | tf_op jit(solution)/shard_map/ppermute | solution.py:33

commit v3 on v2

--- a/solution.py
+++ b/solution.py
@@ -78,7 +78,6 @@
 def terms_kernel(
     place_ref, in_ref, wg_ref, wu_ref, wd_ref, theirs_ref, mine_ref, ord_ref, prod_ref
 ):
-    j = pl.program_id(0)
     steps = wg_ref.shape[1] // LANES
     peers = theirs_ref.shape[0]
     sources, rows2, depth = in_ref.shape
@@ -89,48 +88,47 @@
     width = steps * part
     core = place_ref[0]
     sides = ((1 - core, theirs_ref), (core, mine_ref))
-
-    @pl.when(j == 0)
-    def _():
-        for at, side in ((0, 1 - core), (half, core)):
-            own = in_ref[pl.ds(side * (sources // 2), sources // 2), rows:, :]
-            ord_ref[at : at + half] = own.reshape(half, depth)
-
-    last = pl.multiple_of(jnp.maximum(j - 1, 0) * part, part)
-    for side, out_ref in sides:
-        token_at = pl.multiple_of(side * half, half)
-        block = prod_ref[lax.rem(j + 1, 2), pl.ds(token_at, half), :].T.astype(BF16)
-        out_ref[:, pl.ds(last, part), :] = block[:LANES].reshape(peers, part, half)
-        out_ref[:, pl.ds(width + last, part), :] = block[LANES:].reshape(peers, part, half)
     x = in_ref[:, :rows, :].reshape(tokens, depth)
-    now = pl.multiple_of(jnp.minimum(j, steps - 1) * LANES, LANES)
-    w = jnp.concatenate([wg_ref[:, pl.ds(now, LANES)], wu_ref[:, pl.ds(now, LANES)]], 1)
-    prod_ref[lax.rem(j, 2)] = jnp.dot(x, w, preferred_element_type=F32)
-
-    @pl.when(j == steps)
-    def _():
-        for first in range(0, steps, 4):
-            end = min(first + 4, steps)
-            rows_in = slice(first * LANES, end * LANES)
-            block = dot(wd_ref[rows_in], ord_ref[...], (1, 1)).astype(BF16)
-            for step in range(first, end):
-                piece = block[(step - first) * LANES : (step - first + 1) * LANES]
-                piece = piece.reshape(peers, part, tokens)
-                to = 2 * width + step * part
-                theirs_ref[:, to : to + part, :] = piece[:, :, :half]
-                mine_ref[:, to : to + part, :] = piece[:, :, half:]
+
+    def multiply(step):
+        lanes = slice(step * LANES, (step + 1) * LANES)
+        w = jnp.concatenate([wg_ref[:, lanes], wu_ref[:, lanes]], 1)
+        prod_ref[step % 2] = jnp.dot(x, w, preferred_element_type=F32)
+
+    def turn(step):
+        at = step * part
+        for side, out_ref in sides:
+            token_at = pl.multiple_of(side * half, half)
+            block = prod_ref[step % 2, pl.ds(token_at, half), :].T.astype(BF16)
+            out_ref[:, at : at + part, :] = block[:LANES].reshape(peers, part, half)
+            out_ref[:, width + at : width + at + part, :] = block[LANES:].reshape(peers, part, half)
+
+    for step in range(steps):
+        multiply(step)
+        if step:
+            turn(step - 1)
+    for at, side in ((0, 1 - core), (half, core)):
+        own = in_ref[pl.ds(side * (sources // 2), sources // 2), rows:, :]
+        ord_ref[at : at + half] = own.reshape(half, depth)
+    turn(steps - 1)
+    for first in range(0, steps, 4):
+        end = min(first + 4, steps)
+        block = dot(wd_ref[first * LANES : end * LANES], ord_ref[...], (1, 1)).astype(BF16)
+        for step in range(first, end):
+            piece = block[(step - first) * LANES : (step - first + 1) * LANES]
+            piece = piece.reshape(peers, part, tokens)
+            to = 2 * width + step * part
+            theirs_ref[:, to : to + part, :] = piece[:, :, :half]
+            mine_ref[:, to : to + part, :] = piece[:, :, half:]
 
 
 def terms(place, fetched, w_gate, w_up, w_down, peers):
     depth, hidden = w_gate.shape
     tokens = fetched.shape[0] * fetched.shape[1] // 2
-    steps = hidden // LANES
-    rows = 3 * hidden // peers
-    out = jax.ShapeDtypeStruct((peers, rows, tokens // 2), BF16)
+    out = jax.ShapeDtypeStruct((peers, 3 * hidden // peers, tokens // 2), BF16)
     dy = jax.ShapeDtypeStruct((tokens, depth), BF16)
     return pl.pallas_call(
         terms_kernel,
-        grid=(steps + 1,),
         in_specs=[SMEM] + [VMEM] * 4,
         out_specs=[VMEM] * 3,
         out_shape=[out, out, dy],
@@ -251,7 +249,7 @@
         pair = ends_ref[peer, width:].astype(F32)
         total = total + (pair[:SUBLANES] + pair[SUBLANES:])
     scale = radius_ref[...] * lax.rsqrt(total + 1e-06)
-    norm_ref[...] = jnp.sqrt(total)
+    norm_ref[...] = jnp.sqrt(total)[:1, :1]
     scale_ref[...] = scale
     pgate = gate_ref[...] + scale[:1] * step_ref[:width]
     pup = up_ref[...] + scale[:1] * step_ref[width:]
@@ -265,50 +263,35 @@
 ):
     peers, width, half = pm_ref.shape
     part = LANES // peers
-
-    @pl.when(pl.program_id(0) == 0)
-    def _():
-        for at, p_ref in ((0, pt_ref), (half, pm_ref)):
-            for j in range(width // part):
-                block = p_ref[:, j * part : (j + 1) * part, :].reshape(LANES, half)
-                ph_ref[at : at + half, j * LANES : (j + 1) * LANES] = (
-                    block.astype(F32).T.astype(BF16)
-                )
-        for a, p_ref in ((0, pt_ref), (half, pm_ref)):
-            for b, h_ref in ((0, ht_ref), (half, hm_ref)):
-                p = p_ref[...].reshape(peers * width, half)
-                h = h_ref[:, :width, :].reshape(peers * width, half)
-                mix = scale_ref[:1] * dot(p, h, (0, 0))
-                mix_ref[a : a + half, b : b + half] = mix.astype(BF16)
-
-    acc = dot(ph_ref[...], wd_ref[...], (1, 0)) + dot(mix_ref[...], dy_ref[...], (1, 0))
-    out = acc.astype(BF16)
+    for a, p_ref in ((0, pt_ref), (half, pm_ref)):
+        for b, h_ref in ((0, ht_ref), (half, hm_ref)):
+            p = p_ref[...].reshape(peers * width, half)
+            h = h_ref[:, :width, :].reshape(peers * width, half)
+            mix = scale_ref[:1] * dot(p, h, (0, 0))
+            mix_ref[a : a + half, b : b + half] = mix.astype(BF16)
+    for at, p_ref in ((0, pt_ref), (half, pm_ref)):
+        for j in range(width // part):
+            block = p_ref[:, j * part : (j + 1) * part, :].reshape(LANES, half)
+            ph_ref[at : at + half, j * LANES : (j + 1) * LANES] = block.astype(F32).T.astype(BF16)
     theirs = pl.multiple_of((1 - place_ref[0]) * half, half)
     mine = pl.multiple_of(place_ref[0] * half, half)
-    out_ref[pl.ds(theirs, half), :] = out[:half]
-    out_ref[pl.ds(mine, half), :] = out[half:]
+    depth = dy_ref.shape[1]
+    block = min(depth, 256)
+    for first in range(0, depth, block):
+        lanes = slice(first, first + block)
+        acc = dot(ph_ref[...], wd_ref[:, lanes], (1, 0)) + dot(mix_ref[...], dy_ref[:, lanes], (1, 0))
+        out = acc.astype(BF16)
+        out_ref[pl.ds(theirs, half), lanes] = out[:half]
+        out_ref[pl.ds(mine, half), lanes] = out[half:]
 
 
 def out_terms(place, scale, ph_theirs, ph_mine, h_theirs, h_mine, w_down, dy):
     hidden, depth = w_down.shape
     tokens = dy.shape[0]
-    block = min(depth, 256)
-    ph_spec = pl.BlockSpec(ph_mine.shape, lambda n: (0, 0, 0))
-    h_spec = pl.BlockSpec(h_mine.shape, lambda n: (0, 0, 0))
     return pl.pallas_call(
         out_kernel,
-        grid=(depth // block,),
-        in_specs=[
-            SMEM,
-            pl.BlockSpec(scale.shape, lambda n: (0, 0)),
-            ph_spec,
-            ph_spec,
-            h_spec,
-            h_spec,
-            pl.BlockSpec((hidden, block), lambda n: (0, n)),
-            pl.BlockSpec((tokens, block), lambda n: (0, n)),
-        ],
-        out_specs=pl.BlockSpec((tokens, block), lambda n: (0, n)),
+        in_specs=[SMEM] + [VMEM] * 7,
+        out_specs=VMEM,
         out_shape=jax.ShapeDtypeStruct((tokens, depth), BF16),
         scratch_shapes=[pltpu.VMEM((tokens, hidden), BF16), pltpu.VMEM((tokens, tokens), BF16)],
         compiler_params=pltpu.CompilerParams(vmem_limit_bytes=24 * MIB),
@@ -389,14 +372,16 @@
     h_mine = exchange(sent, Z)
     tile = ((SUBLANES, half), F32)
     sent, scale, norm = local_kernel(
-        pert_kernel, [((peers, width, half), BF16), tile, tile], (h_mine, gate, up, step, radius)
+        pert_kernel,
+        [((peers, width, half), BF16), tile, ((1, 1), F32)],
+        (h_mine, gate, up, step, radius),
     )
     ph_mine = exchange(sent, Z)
     ph_mine, h_mine = lax.optimization_barrier((ph_mine, h_mine))
     ph_theirs = swap_cores(ph_mine)
     h_theirs = swap_cores(h_mine)
     partial_out = out_terms(place, scale, ph_theirs, ph_mine, h_theirs, h_mine, w_down, dy)
-    partial_out, norm = lax.optimization_barrier((partial_out, norm[0, :1]))
+    partial_out, norm = lax.optimization_barrier((partial_out, norm.reshape(1)))
     parts = exchange(partial_out.reshape(sources, rows, depth), ROW)
     return (jnp.sum(parts.astype(F32), 0).astype(BF16), norm)
 

time: 172 us -> 168 us (0.977)
  Pallas kernels: 14 us -> 10.4 us
    pallas_call x2, Pallas kernels: 10.1 us -> 6.08 us  [the longest x1 3.63 us: terms(): pl.pallas_call(terms_kernel, in_specs=[SMEM] + [VMEM] * 4, out_specs=[VME...]
  transfers between devices with their start and end apart: 14 -> 14, of which waited for: 7 -> 7; matrix products, arithmetic and copies ran while one was open for 0% -> 0% of each run, Pallas kernels for 4% -> 2%
where the time goes in v3:
time: 168 us
  blocking collectives  96.6 us (58%)
  starting transfers between devices  31.3 us (19%)
  waiting for transfers between devices  25.8 us (15%)
  Pallas kernels  10.4 us (6%)
    all_to_all x6, blocking collectives, exchange(): return lax.all_to_all(x, axis, 0, 0, tiled=True)  96.6 us
    ppermute x6, starting transfers between devices, moved(): return lax.ppermute(x, Z, [(z, (z + by) % peers) for z in range(peers)])  13.8 us
    ppermute x6, waiting for transfers between devices, moved(): return lax.ppermute(x, Z, [(z, (z + by) % peers) for z in range(peers)])  12.4 us
    ppermute x1, waiting for transfers between devices, per_device(): second = lax.ppermute(second, Z, other)  7.32 us
    ppermute x5, starting transfers between devices, swap_cores(): return lax.ppermute(x, CORE, [(0, 1), (1, 0)])  6.47 us
    ppermute x5, waiting for transfers between devices, swap_cores(): return lax.ppermute(x, CORE, [(0, 1), (1, 0)])  5.02 us
    ppermute x1, starting transfers between devices, per_device(): theirs = lax.ppermute(gram, Z, neighbour)  4.68 us
    ppermute x1, starting transfers between devices, per_device(): second = lax.ppermute(second, Z, other)  4.67 us
  transfers between devices with their start and end apart: 14, of which 7 were waited for; matrix products, arithmetic and copies ran while one was open for 0% of the time, Pallas kernels for 2%

profile of v3, /device:TPU:1, one launch (start us, length us, event | category | flops | bytes accessed | tf_op | source)
XLA Modules:
  0.0 167.7 jit_solution(9867582600203800494)
XLA Ops:
  1.3 0.1 pad_add_fusion.place_ref
  1.4 0.0 copy-start.3
  1.4 0.8 copy-done.3
  2.1 0.0 copy-start.4
  2.1 0.8 copy-done.4
  2.9 0.0 copy-start
  2.9 0.0 copy-start.1
  2.9 0.0 copy-start.2
  2.9 0.2 copies_in.1
  3.1 23.7 %all_to_all.30.in_ref = bf16[16,32,1024]{2,1,0:T(8,128)(2,1)S(1)} all-to-all(bf16[16,32,1024]{2,1,0:T(8,128)(2,1)S(1)} %copies_in.1), channel_id=1, replica_groups=mesh['row_0'=4,'row_1'=4,'col_0'=8,'col_1'=2] {'row_0','row_1'}, dimensions={0} | all-to-all | bytes 2097152 | tf_op jit(solution)/shard_map/all_to_all | solution.py:29
  26.8 0.9 shard_map.80
  27.7 2.1 %collective-permute-start = (bf16[32,128]{1,0:T(8,128)(2,1)S(1)}, bf16[32,128]{1,0:T(8,128)(2,1)S(1)}, u32[]{:S(2)}, u32[]{:S(2)}) collective-permute-start(bf16[32,128]{1,0:T(8,128)(2,1)S(1)} %get-tuple-element.42), channel_id=1, source_target_pairs={{0,1},{1,0},{2,3},{3,2},{4,5},{5,4},{6,7},{7,6},{8,9},{9,8},{10,11... | collective-permute-start | bytes 24584 | tf_op jit(solution)/shard_map/ppermute | solution.py:33
  29.8 0.0 copy-done
  29.8 0.0 copy-done.1
  29.8 0.0 copy-done.2
  29.8 3.6 %terms.1 = (bf16[8,624,128]{2,1,0:T(8,128)(2,1)S(1)}, bf16[8,624,128]{2,1,0:T(8,128)(2,1)S(1)}, bf16[256,1024]{1,0:T(8,128)(2,1)S(1)}) custom-call(s32[3]{0:T(128)S(1)} %pad_add_fusion.place_ref, bf16[16,32,1024]{2,1,0:T(8,128)(2,1)S(1)} %all_to_all.30.in_ref, bf16[1024,1664]{1,0:T(8,128)(2,1)S(1)} %copy-done.1, bf16[1024,1664]{1,0:T(8,128)(2,1)S(1)} %copy-done.2, ...), custom_call_target="tpu_custom_call" | custom-call | flops 2617245696 | bytes 10223616 | tf_op jit(solution)/shard_map/terms/pallas_call | solution.py:130
  33.4 0.0 collective-permute-done.refs_1_
  33.4 0.1 collective-permute-start.1
  33.5 3.0 %collective-permute-done.1.arrived_ref = bf16[8,624,128]{2,1,0:T(8,128)(2,1)S(1)} collective-permute-done((bf16[8,624,128]{2,1,0:T(8,128)(2,1)S(1)}, bf16[8,624,128]{2,1,0:T(8,128)(2,1)S(1)}, u32[]{:S(2)}, u32[]{:S(2)}) %collective-permute-start.1) | collective-permute-done | bytes 1277984 | tf_op jit(solution)/shard_map/ppermute | solution.py:33
  36.5 0.8 shard_map.82
  37.3 1.7 %collective-permute-start.2 = (bf16[4,320,128]{2,1,0:T(8,128)(2,1)S(1)}, bf16[4,320,128]{2,1,0:T(8,128)(2,1)S(1)}, u32[]{:S(2)}, u32[]{:S(2)}) collective-permute-start(bf16[4,320,128]{2,1,0:T(8,128)(2,1)S(1)} %get-tuple-element.45), channel_id=1, source_target_pairs={{0,2},{2,0},{4,6},{6,4},{8,10},{10,8},{12,14},{14,12},{1,3},{3,1},... | collective-permute-start | bytes 983048 | tf_op jit(solution)/shard_map/ppermute | solution.py:342
  39.1 4.7 %collective-permute-start.3 = (bf16[4,304,128]{2,1,0:T(8,128)(2,1)S(1)}, bf16[4,304,128]{2,1,0:T(8,128)(2,1)S(1)}, u32[]{:S(2)}, u32[]{:S(2)}) collective-permute-start(bf16[4,304,128]{2,1,0:T(8,128)(2,1)S(1)} %get-tuple-element.46), channel_id=1, source_target_pairs={{0,14},{2,4},{4,2},{6,8},{8,6},{10,12},{12,10},{14,0},{1,15},{3,5}... | collective-permute-start | bytes 933896 | tf_op jit(solution)/shard_map/ppermute | solution.py:343
  43.7 7.3 %collective-permute-done.3.second_ref = bf16[4,304,128]{2,1,0:T(8,128)(2,1)S(1)} collective-permute-done((bf16[4,304,128]{2,1,0:T(8,128)(2,1)S(1)}, bf16[4,304,128]{2,1,0:T(8,128)(2,1)S(1)}, u32[]{:S(2)}, u32[]{:S(2)}) %collective-permute-start.3) | collective-permute-done | bytes 311328 | tf_op jit(solution)/shard_map/ppermute | solution.py:343
  51.0 0.0 collective-permute-done.2.first_ref
  51.0 0.7 shard_map.83
  51.7 0.1 collective-permute-start.4
  51.8 3.6 %collective-permute-start.5 = (bf16[624,128]{1,0:T(8,128)(2,1)S(1)}, bf16[624,128]{1,0:T(8,128)(2,1)S(1)}, u32[]{:S(2)}, u32[]{:S(2)}) collective-permute-start(bf16[624,128]{1,0:T(8,128)(2,1)S(1)} %get-tuple-element.49), channel_id=1, source_target_pairs={{0,12},{2,14},{4,0},{6,2},{8,4},{10,6},{12,8},{14,10},{1,13},{3,15... | collective-permute-start | bytes 479240 | tf_op jit(solution)/shard_map/ppermute | solution.py:317
  55.4 3.7 %collective-permute-start.6 = (bf16[624,128]{1,0:T(8,128)(2,1)S(1)}, bf16[624,128]{1,0:T(8,128)(2,1)S(1)}, u32[]{:S(2)}, u32[]{:S(2)}) collective-permute-start(bf16[624,128]{1,0:T(8,128)(2,1)S(1)} %get-tuple-element.50), channel_id=1, source_target_pairs={{0,8},{2,10},{4,12},{6,14},{8,0},{10,2},{12,4},{14,6},{1,9},{3,11}... | collective-permute-start | bytes 479240 | tf_op jit(solution)/shard_map/ppermute | solution.py:317
  59.1 1.4 collective-permute-done.4.up_in
  60.6 7.3 %collective-permute-done.5.down_in = bf16[624,128]{1,0:T(8,128)(2,1)S(1)} collective-permute-done((bf16[624,128]{1,0:T(8,128)(2,1)S(1)}, bf16[624,128]{1,0:T(8,128)(2,1)S(1)}, u32[]{:S(2)}, u32[]{:S(2)}) %collective-permute-start.5) | collective-permute-done | bytes 159776 | tf_op jit(solution)/shard_map/ppermute | solution.py:317
  67.9 0.0 collective-permute-done.6.far_in
  67.9 0.1 shard_map.84
  68.0 0.9 collective-permute-start.7
  68.9 4.7 %collective-permute-start.8 = (bf16[32,128]{1,0:T(8,128)(2,1)S(1)}, bf16[32,128]{1,0:T(8,128)(2,1)S(1)}, u32[]{:S(2)}, u32[]{:S(2)}) collective-permute-start(bf16[32,128]{1,0:T(8,128)(2,1)S(1)} %shard_map.81.refs_0_), channel_id=1, source_target_pairs={{0,2},{2,0},{4,6},{6,4},{8,10},{10,8},{12,14},{14,12},{1,3},{3,1},... | collective-permute-start | bytes 24584 | tf_op jit(solution)/shard_map/ppermute | solution.py:331
  73.6 1.0 collective-permute-done.8.refs_1_
  74.7 2.8 %collective-permute-start.9 = (bf16[32,128]{1,0:T(8,128)(2,1)S(1)}, bf16[32,128]{1,0:T(8,128)(2,1)S(1)}, u32[]{:S(2)}, u32[]{:S(2)}) collective-permute-start(bf16[32,128]{1,0:T(8,128)(2,1)S(1)} %shard_map.85.refs_0_), channel_id=1, source_target_pairs={{0,4},{2,6},{4,8},{6,10},{8,12},{10,14},{12,0},{14,2},{1,5},{3,7},... | collective-permute-start | bytes 24584 | tf_op jit(solution)/shard_map/ppermute | solution.py:317
  77.4 0.8 collective-permute-start.10
  78.2 2.8 %collective-permute-start.11 = (bf16[32,128]{1,0:T(8,128)(2,1)S(1)}, bf16[32,128]{1,0:T(8,128)(2,1)S(1)}, u32[]{:S(2)}, u32[]{:S(2)}) collective-permute-start(bf16[32,128]{1,0:T(8,128)(2,1)S(1)} %shard_map.85.refs_0_), channel_id=1, source_target_pairs={{0,8},{2,10},{4,12},{6,14},{8,0},{10,2},{12,4},{14,6},{1,9},{3,11}... | collective-permute-start | bytes 24584 | tf_op jit(solution)/shard_map/ppermute | solution.py:317
  81.0 0.0 collective-permute-done.9.refs_1_
  81.0 0.0 collective-permute-done.10.refs_2_
  81.0 3.6 %collective-permute-done.11.refs_3_ = bf16[32,128]{1,0:T(8,128)(2,1)S(1)} collective-permute-done((bf16[32,128]{1,0:T(8,128)(2,1)S(1)}, bf16[32,128]{1,0:T(8,128)(2,1)S(1)}, u32[]{:S(2)}, u32[]{:S(2)}) %collective-permute-start.11) | collective-permute-done | bytes 8224 | tf_op jit(solution)/shard_map/ppermute | solution.py:317
  84.7 9.5 %all_to_all.31.parts_ref = bf16[16,32,128]{2,1,0:T(8,128)(2,1)S(1)} all-to-all(bf16[16,32,128]{2,1,0:T(8,128)(2,1)S(1)} %shard_map.86), channel_id=1, replica_groups=mesh['row_0'=4,'row_1'=4,'col_0'=8,'col_1'=2] {'row_0','row_1'}, dimensions={0} | all-to-all | bytes 262144 | tf_op jit(solution)/shard_map/all_to_all | solution.py:29
  94.2 0.0 collective-permute-done.7.arrived_ref
  94.2 0.9 shard_map.88
  95.1 14.8 %all_to_all.32.plane_ref = f32[32,8,128]{2,1,0:T(8,128)S(1)} all-to-all(f32[32,8,128]{2,1,0:T(8,128)S(1)} %get-tuple-element.53), channel_id=1, replica_groups=mesh['row_0'=4,'row_1'=4,'col_0'=8,'col_1'=2] {'row_0','row_1','col_1'}, dimensions={0} | all-to-all | bytes 262144 | tf_op jit(solution)/shard_map/all_to_all | solution.py:29
  110.0 0.1 shard_map.89
  110.0 19.6 %all_to_all.33.ends_ref.hm_ref = bf16[8,224,128]{2,1,0:T(8,128)(2,1)S(1)} all-to-all(bf16[8,224,128]{2,1,0:T(8,128)(2,1)S(1)} %shard_map.89), channel_id=1, replica_groups=mesh['row_0'=4,'row_1'=4,'col_0'=8,'col_1'=2] {'col_0'}, dimensions={0} | all-to-all | bytes 917504 | tf_op jit(solution)/shard_map/all_to_all | solution.py:29
  129.7 0.5 shard_map.90
  130.2 15.3 %all_to_all.34.pm_ref = bf16[8,208,128]{2,1,0:T(8,128)(2,1)S(1)} all-to-all(bf16[8,208,128]{2,1,0:T(8,128)(2,1)S(1)} %get-tuple-element.59), channel_id=1, replica_groups=mesh['row_0'=4,'row_1'=4,'col_0'=8,'col_1'=2] {'col_0'}, dimensions={0} | all-to-all | bytes 851968 | tf_op jit(solution)/shard_map/all_to_all | solution.py:29
  145.5 3.4 %collective-permute-start.13 = (bf16[8,224,128]{2,1,0:T(8,128)(2,1)S(1)}, bf16[8,224,128]{2,1,0:T(8,128)(2,1)S(1)}, u32[]{:S(2)}, u32[]{:S(2)}) collective-permute-start(bf16[8,224,128]{2,1,0:T(8,128)(2,1)S(1)} %all_to_all.33.ends_ref.hm_ref), channel_id=1, source_target_pairs={{0,1},{1,0},{2,3},{3,2},{4,5},{5,4},{6,7},{7,6},{8,9},{9,8},{10,11... | collective-permute-start | bytes 1376264 | tf_op jit(solution)/shard_map/ppermute | solution.py:33
  148.9 0.0 collective-permute-start.12
  148.9 2.0 %collective-permute-done.12.pt_ref = bf16[8,208,128]{2,1,0:T(8,128)(2,1)S(1)} collective-permute-done((bf16[8,208,128]{2,1,0:T(8,128)(2,1)S(1)}, bf16[8,208,128]{2,1,0:T(8,128)(2,1)S(1)}, u32[]{:S(2)}, u32[]{:S(2)}) %collective-permute-start.12) | collective-permute-done | bytes 426016 | tf_op jit(solution)/shard_map/ppermute | solution.py:33
  151.0 0.0 collective-permute-done.13.ht_ref
  151.0 2.5 %out_terms.1 = bf16[256,1024]{1,0:T(8,128)(2,1)S(1)} custom-call(s32[3]{0:T(128)S(1)} %pad_add_fusion.place_ref, f32[8,128]{1,0:T(8,128)S(1)} %get-tuple-element.58.scale_ref, bf16[8,208,128]{2,1,0:T(8,128)(2,1)S(1)} %collective-permute-done.12.pt_ref, bf16[8,208,128]{2,1,0:T(8,128)(2,1)S(1)} %all_to_all.34.pm_ref, ...), custom_call_target="tpu_custom_call" | custom-call | flops 872415232 | bytes 3407872 | tf_op jit(solution)/shard_map/out_terms/pallas_call | solution.py:291
  153.4 13.6 %all_to_all.35 = bf16[16,16,1024]{2,1,0:T(8,128)(2,1)S(1)} all-to-all(bf16[16,16,1024]{2,1,0:T(8,128)(2,1)S(1)} %bitcast.7), channel_id=1, replica_groups=mesh['row_0'=4,'row_1'=4,'col_0'=8,'col_1'=2] {'row_0','row_1'}, dimensions={0} | all-to-all | bytes 1048576 | tf_op jit(solution)/shard_map/all_to_all | solution.py:29
  167.0 0.7 reduce_sum.12
  (5 shorter events, 0.0 us)
Async XLA Ops:
  1.4 0.8 copy-start.3
  2.1 0.8 copy-start.4
  2.9 26.9 %copy-start = (bf16[1664,1024]{1,0:T(8,128)(2,1)S(1)}, bf16[1664,1024]{1,0:T(8,128)(2,1)}, u32[]{:S(2)}) copy-start(bf16[1664,1024]{1,0:T(8,128)(2,1)} %wd_ref.3) | copy-start | bytes 10223620
  2.9 26.9 %copy-start.1 = (bf16[1024,1664]{1,0:T(8,128)(2,1)S(1)}, bf16[1024,1664]{1,0:T(8,128)(2,1)}, u32[]{:S(2)}) copy-start(bf16[1024,1664]{1,0:T(8,128)(2,1)} %wg_ref.1) | copy-start | bytes 10223620
  2.9 26.9 %copy-start.2 = (bf16[1024,1664]{1,0:T(8,128)(2,1)S(1)}, bf16[1024,1664]{1,0:T(8,128)(2,1)}, u32[]{:S(2)}) copy-start(bf16[1024,1664]{1,0:T(8,128)(2,1)} %wu_ref.1) | copy-start | bytes 10223620
  27.7 5.7 %collective-permute-start = (bf16[32,128]{1,0:T(8,128)(2,1)S(1)}, bf16[32,128]{1,0:T(8,128)(2,1)S(1)}, u32[]{:S(2)}, u32[]{:S(2)}) collective-permute-start(bf16[32,128]{1,0:T(8,128)(2,1)S(1)} %get-tuple-element.42), channel_id=1, source_target_pairs={{0,1},{1,0},{2,3},{3,2},{4,5},{5,4},{6,7},{7,6},{8,9},{9,8},{10,11... | collective-permute-start | bytes 24584 | tf_op jit(solution)/shard_map/ppermute | solution.py:33
  33.4 3.1 %collective-permute-start.1 = (bf16[8,624,128]{2,1,0:T(8,128)(2,1)S(1)}, bf16[8,624,128]{2,1,0:T(8,128)(2,1)S(1)}, u32[]{:S(2)}, u32[]{:S(2)}) collective-permute-start(bf16[8,624,128]{2,1,0:T(8,128)(2,1)S(1)} %get-tuple-element.43), channel_id=1, source_target_pairs={{0,1},{1,0},{2,3},{3,2},{4,5},{5,4},{6,7},{7,6},{8,9},{9,8},{10,11... | collective-permute-start | bytes 3833864 | tf_op jit(solution)/shard_map/ppermute | solution.py:33
  37.3 13.7 %collective-permute-start.2 = (bf16[4,320,128]{2,1,0:T(8,128)(2,1)S(1)}, bf16[4,320,128]{2,1,0:T(8,128)(2,1)S(1)}, u32[]{:S(2)}, u32[]{:S(2)}) collective-permute-start(bf16[4,320,128]{2,1,0:T(8,128)(2,1)S(1)} %get-tuple-element.45), channel_id=1, source_target_pairs={{0,2},{2,0},{4,6},{6,4},{8,10},{10,8},{12,14},{14,12},{1,3},{3,1},... | collective-permute-start | bytes 983048 | tf_op jit(solution)/shard_map/ppermute | solution.py:342
  39.1 12.0 %collective-permute-start.3 = (bf16[4,304,128]{2,1,0:T(8,128)(2,1)S(1)}, bf16[4,304,128]{2,1,0:T(8,128)(2,1)S(1)}, u32[]{:S(2)}, u32[]{:S(2)}) collective-permute-start(bf16[4,304,128]{2,1,0:T(8,128)(2,1)S(1)} %get-tuple-element.46), channel_id=1, source_target_pairs={{0,14},{2,4},{4,2},{6,8},{8,6},{10,12},{12,10},{14,0},{1,15},{3,5}... | collective-permute-start | bytes 933896 | tf_op jit(solution)/shard_map/ppermute | solution.py:343
  51.7 8.8 %collective-permute-start.4 = (bf16[624,128]{1,0:T(8,128)(2,1)S(1)}, bf16[624,128]{1,0:T(8,128)(2,1)S(1)}, u32[]{:S(2)}, u32[]{:S(2)}) collective-permute-start(bf16[624,128]{1,0:T(8,128)(2,1)S(1)} %get-tuple-element.48), channel_id=1, source_target_pairs={{0,4},{2,6},{4,8},{6,10},{8,12},{10,14},{12,0},{14,2},{1,5},{3,7},... | collective-permute-start | bytes 479240 | tf_op jit(solution)/shard_map/ppermute | solution.py:317
  51.8 16.1 %collective-permute-start.5 = (bf16[624,128]{1,0:T(8,128)(2,1)S(1)}, bf16[624,128]{1,0:T(8,128)(2,1)S(1)}, u32[]{:S(2)}, u32[]{:S(2)}) collective-permute-start(bf16[624,128]{1,0:T(8,128)(2,1)S(1)} %get-tuple-element.49), channel_id=1, source_target_pairs={{0,12},{2,14},{4,0},{6,2},{8,4},{10,6},{12,8},{14,10},{1,13},{3,15... | collective-permute-start | bytes 479240 | tf_op jit(solution)/shard_map/ppermute | solution.py:317
  55.4 12.5 %collective-permute-start.6 = (bf16[624,128]{1,0:T(8,128)(2,1)S(1)}, bf16[624,128]{1,0:T(8,128)(2,1)S(1)}, u32[]{:S(2)}, u32[]{:S(2)}) collective-permute-start(bf16[624,128]{1,0:T(8,128)(2,1)S(1)} %get-tuple-element.50), channel_id=1, source_target_pairs={{0,8},{2,10},{4,12},{6,14},{8,0},{10,2},{12,4},{14,6},{1,9},{3,11}... | collective-permute-start | bytes 479240 | tf_op jit(solution)/shard_map/ppermute | solution.py:317
  68.0 26.1 %collective-permute-start.7 = (bf16[624,128]{1,0:T(8,128)(2,1)S(1)}, bf16[624,128]{1,0:T(8,128)(2,1)S(1)}, u32[]{:S(2)}, u32[]{:S(2)}) collective-permute-start(bf16[624,128]{1,0:T(8,128)(2,1)S(1)} %get-tuple-element.51.acts_ref), channel_id=1, source_target_pairs={{0,1},{1,0},{2,3},{3,2},{4,5},{5,4},{6,7},{7,6},{8,9},{9,8},{10,11... | collective-permute-start | bytes 479240 | tf_op jit(solution)/shard_map/ppermute | solution.py:33
  68.9 5.7 %collective-permute-start.8 = (bf16[32,128]{1,0:T(8,128)(2,1)S(1)}, bf16[32,128]{1,0:T(8,128)(2,1)S(1)}, u32[]{:S(2)}, u32[]{:S(2)}) collective-permute-start(bf16[32,128]{1,0:T(8,128)(2,1)S(1)} %shard_map.81.refs_0_), channel_id=1, source_target_pairs={{0,2},{2,0},{4,6},{6,4},{8,10},{10,8},{12,14},{14,12},{1,3},{3,1},... | collective-permute-start | bytes 24584 | tf_op jit(solution)/shard_map/ppermute | solution.py:331
  74.7 6.4 %collective-permute-start.9 = (bf16[32,128]{1,0:T(8,128)(2,1)S(1)}, bf16[32,128]{1,0:T(8,128)(2,1)S(1)}, u32[]{:S(2)}, u32[]{:S(2)}) collective-permute-start(bf16[32,128]{1,0:T(8,128)(2,1)S(1)} %shard_map.85.refs_0_), channel_id=1, source_target_pairs={{0,4},{2,6},{4,8},{6,10},{8,12},{10,14},{12,0},{14,2},{1,5},{3,7},... | collective-permute-start | bytes 24584 | tf_op jit(solution)/shard_map/ppermute | solution.py:317
  77.4 3.6 %collective-permute-start.10 = (bf16[32,128]{1,0:T(8,128)(2,1)S(1)}, bf16[32,128]{1,0:T(8,128)(2,1)S(1)}, u32[]{:S(2)}, u32[]{:S(2)}) collective-permute-start(bf16[32,128]{1,0:T(8,128)(2,1)S(1)} %shard_map.85.refs_0_), channel_id=1, source_target_pairs={{0,12},{2,14},{4,0},{6,2},{8,4},{10,6},{12,8},{14,10},{1,13},{3,15... | collective-permute-start | bytes 24584 | tf_op jit(solution)/shard_map/ppermute | solution.py:317
  78.2 6.4 %collective-permute-start.11 = (bf16[32,128]{1,0:T(8,128)(2,1)S(1)}, bf16[32,128]{1,0:T(8,128)(2,1)S(1)}, u32[]{:S(2)}, u32[]{:S(2)}) collective-permute-start(bf16[32,128]{1,0:T(8,128)(2,1)S(1)} %shard_map.85.refs_0_), channel_id=1, source_target_pairs={{0,8},{2,10},{4,12},{6,14},{8,0},{10,2},{12,4},{14,6},{1,9},{3,11}... | collective-permute-start | bytes 24584 | tf_op jit(solution)/shard_map/ppermute | solution.py:317
  145.5 5.4 %collective-permute-start.13 = (bf16[8,224,128]{2,1,0:T(8,128)(2,1)S(1)}, bf16[8,224,128]{2,1,0:T(8,128)(2,1)S(1)}, u32[]{:S(2)}, u32[]{:S(2)}) collective-permute-start(bf16[8,224,128]{2,1,0:T(8,128)(2,1)S(1)} %all_to_all.33.ends_ref.hm_ref), channel_id=1, source_target_pairs={{0,1},{1,0},{2,3},{3,2},{4,5},{5,4},{6,7},{7,6},{8,9},{9,8},{10,11... | collective-permute-start | bytes 1376264 | tf_op jit(solution)/shard_map/ppermute | solution.py:33
  148.9 2.1 %collective-permute-start.12 = (bf16[8,208,128]{2,1,0:T(8,128)(2,1)S(1)}, bf16[8,208,128]{2,1,0:T(8,128)(2,1)S(1)}, u32[]{:S(2)}, u32[]{:S(2)}) collective-permute-start(bf16[8,208,128]{2,1,0:T(8,128)(2,1)S(1)} %all_to_all.34.pm_ref), channel_id=1, source_target_pairs={{0,1},{1,0},{2,3},{3,2},{4,5},{5,4},{6,7},{7,6},{8,9},{9,8},{10,11... | collective-permute-start | bytes 1277960 | tf_op jit(solution)/shard_map/ppermute | solution.py:33

commit v4 on v3

--- a/solution.py
+++ b/solution.py
@@ -44,35 +44,24 @@
     )(*operands)
 
 
-def copies_in_kernel(tokens_ref, dy_ref, out_ref, done):
-    rows = tokens_ref.shape[0]
-    copies = [
-        pltpu.make_async_copy(
-            own_ref, out_ref.at[0, kind * rows : (kind + 1) * rows], done.at[kind]
-        )
-        for kind, own_ref in enumerate((tokens_ref, dy_ref))
-    ]
-    for copy in copies:
-        copy.start()
-    for copy in copies:
-        copy.wait()
-    both = out_ref[0]
-    for peer in range(1, out_ref.shape[0]):
+def copies_in_kernel(both_ref, out_ref):
+    both = both_ref[...]
+    for peer in range(out_ref.shape[0]):
         out_ref[peer] = both
 
 
-def copies_in(tokens, grad_out, sources):
-    rows, depth = tokens.shape
+def copies_in(both, sources):
     return pl.pallas_call(
         copies_in_kernel,
-        in_specs=[pl.BlockSpec(memory_space=pl.ANY)] * 2,
+        in_specs=[VMEM],
         out_specs=VMEM,
-        out_shape=jax.ShapeDtypeStruct((sources, 2 * rows, depth), BF16),
-        scratch_shapes=[pltpu.SemaphoreType.DMA((2,))],
+        out_shape=jax.ShapeDtypeStruct((sources, *both.shape), BF16),
         compiler_params=pltpu.CompilerParams(vmem_limit_bytes=4 * MIB),
-        cost_estimate=pl.CostEstimate(flops=20_000_000_000, bytes_accessed=1_000_000, transcendentals=0),
+        cost_estimate=pl.CostEstimate(
+            flops=20_000_000_000, bytes_accessed=1_000_000, transcendentals=0
+        ),
         name="copies_in",
-    )(tokens, grad_out)
+    )(both)
 
 
 def terms_kernel(
@@ -318,8 +307,9 @@
 
     radius = jnp.broadcast_to(radius, (SUBLANES, half))
     place = jnp.stack([lax.axis_index(axis) for axis in (CORE, Z, ROW)]).astype(jnp.int32)
-    tokens, grad_out, place, radius = lax.optimization_barrier((tokens, grad_out, place, radius))
-    fetched = exchange(copies_in(tokens, grad_out, sources), ROW)
+    both = jnp.concatenate([tokens, grad_out], 0)
+    both, place, radius = lax.optimization_barrier((both, place, radius))
+    fetched = exchange(copies_in(both, sources), ROW)
     flat = ((2 * rows, half), BF16)
     theirs, gram = local_kernel(gram_kernel, [flat, flat], (place, fetched))
     fetched, theirs = lax.optimization_barrier((fetched, theirs))
@@ -377,7 +367,6 @@
         (h_mine, gate, up, step, radius),
     )
     ph_mine = exchange(sent, Z)
-    ph_mine, h_mine = lax.optimization_barrier((ph_mine, h_mine))
     ph_theirs = swap_cores(ph_mine)
     h_theirs = swap_cores(h_mine)
     partial_out = out_terms(place, scale, ph_theirs, ph_mine, h_theirs, h_mine, w_down, dy)

time: 168 us -> 173 us (1.030)
  blocking collectives: 96.6 us -> 81.2 us
  waiting for transfers between devices: 25.8 us -> 37 us
  starting transfers between devices: 31.3 us -> 36.6 us
  local copies, waits for them, and re-layouts: 1.53 us -> 3.62 us
    all_to_all x6 -> x5, blocking collectives: 96.6 us -> 81.2 us  [exchange(): return lax.all_to_all(x, axis, 0, 0, tiled=True)]
    all_to_all x0 -> x1, waiting for transfers between devices: none -> 11.7 us  [exchange(): return lax.all_to_all(x, axis, 0, 0, tiled=True)]
    all_to_all x0 -> x1, starting transfers between devices: none -> 4.11 us  [exchange(): return lax.all_to_all(x, axis, 0, 0, tiled=True)]
    unnamed x10 -> x16, local copies, waits for them, and re-layouts: 1.53 us -> 3.62 us
  transfers between devices with their start and end apart: 14 -> 15, of which waited for: 7 -> 8; matrix products, arithmetic and copies ran while one was open for 0% -> 0% of each run, Pallas kernels for 2% -> 2%
where the time goes in v4:
time: 173 us; the launch traced here: 172 us
  blocking collectives  81.2 us (47%)
  waiting for transfers between devices  37 us (21%)
  starting transfers between devices  36.6 us (21%)
  Pallas kernels  10.7 us (6%)
  local copies, waits for them, and re-layouts  3.62 us (2%)
    all_to_all x5, blocking collectives, exchange(): return lax.all_to_all(x, axis, 0, 0, tiled=True)  81.2 us
    ppermute x6, starting transfers between devices, moved(): return lax.ppermute(x, Z, [(z, (z + by) % peers) for z in range(peers)])  13.8 us
    ppermute x6, waiting for transfers between devices, moved(): return lax.ppermute(x, Z, [(z, (z + by) % peers) for z in range(peers)])  12.4 us
    all_to_all x1, waiting for transfers between devices, exchange(): return lax.all_to_all(x, axis, 0, 0, tiled=True)  11.7 us
    ppermute x5, starting transfers between devices, swap_cores(): return lax.ppermute(x, CORE, [(0, 1), (1, 0)])  7.68 us
    ppermute x1, waiting for transfers between devices, per_device(): second = lax.ppermute(second, Z, other)  7.32 us
    ppermute x1, starting transfers between devices, per_device(): theirs = lax.ppermute(gram, Z, neighbour)  4.68 us
    ppermute x1, starting transfers between devices, per_device(): second = lax.ppermute(second, Z, other)  4.66 us
  transfers between devices with their start and end apart: 15, of which 8 were waited for; matrix products, arithmetic and copies ran while one was open for 0% of the time, Pallas kernels for 2%

profile of v4, /device:TPU:1, one launch (start us, length us, event | category | flops | bytes accessed | tf_op | source)
XLA Modules:
  0.0 172.2 jit_solution(13427598940014864338)
XLA Ops:
  1.3 0.8 pad_maximum_fusion.both_ref
  2.1 0.1 pad_add_fusion.place_ref
  2.1 0.0 copy-start
  2.1 0.0 copy-start.3
  2.1 0.0 copy-start.4
  2.2 0.1 copies_in.1
  2.3 23.7 %all_to_all.30.in_ref = bf16[16,32,1024]{2,1,0:T(8,128)(2,1)S(1)} all-to-all(bf16[16,32,1024]{2,1,0:T(8,128)(2,1)S(1)} %copies_in.1), channel_id=1, replica_groups=mesh['row_0'=4,'row_1'=4,'col_0'=8,'col_1'=2] {'row_0','row_1'}, dimensions={0} | all-to-all | bytes 2097152 | tf_op jit(solution)/shard_map/all_to_all | solution.py:29
  25.9 0.9 shard_map.80
  26.9 2.1 %collective-permute-start = (bf16[32,128]{1,0:T(8,128)(2,1)S(1)}, bf16[32,128]{1,0:T(8,128)(2,1)S(1)}, u32[]{:S(2)}, u32[]{:S(2)}) collective-permute-start(bf16[32,128]{1,0:T(8,128)(2,1)S(1)} %get-tuple-element.38), channel_id=1, source_target_pairs={{0,1},{1,0},{2,3},{3,2},{4,5},{5,4},{6,7},{7,6},{8,9},{9,8},{10,11... | collective-permute-start | bytes 24584 | tf_op jit(solution)/shard_map/ppermute | solution.py:33
  28.9 0.0 copy-done
  28.9 0.0 copy-done.3
  28.9 0.0 copy-done.4
  28.9 3.5 %terms.1 = (bf16[8,624,128]{2,1,0:T(8,128)(2,1)S(1)}, bf16[8,624,128]{2,1,0:T(8,128)(2,1)S(1)}, bf16[256,1024]{1,0:T(8,128)(2,1)S(1)}) custom-call(s32[3]{0:T(128)S(1)} %pad_add_fusion.place_ref, bf16[16,32,1024]{2,1,0:T(8,128)(2,1)S(1)} %all_to_all.30.in_ref, bf16[1024,1664]{1,0:T(8,128)(2,1)S(1)} %copy-done.3, bf16[1024,1664]{1,0:T(8,128)(2,1)S(1)} %copy-done.4, ...), custom_call_target="tpu_custom_call" | custom-call | flops 2617245696 | bytes 10223616 | tf_op jit(solution)/shard_map/terms/pallas_call | solution.py:119
  32.5 0.0 copy-start.5
  32.5 0.0 collective-permute-done.refs_1_
  32.5 0.1 collective-permute-start.1
  32.6 3.0 %collective-permute-done.1.arrived_ref = bf16[8,624,128]{2,1,0:T(8,128)(2,1)S(1)} collective-permute-done((bf16[8,624,128]{2,1,0:T(8,128)(2,1)S(1)}, bf16[8,624,128]{2,1,0:T(8,128)(2,1)S(1)}, u32[]{:S(2)}, u32[]{:S(2)}) %collective-permute-start.1) | collective-permute-done | bytes 1277984 | tf_op jit(solution)/shard_map/ppermute | solution.py:33
  35.6 0.8 shard_map.82
  36.4 0.0 copy-done.5
  36.4 1.7 %collective-permute-start.2 = (bf16[4,320,128]{2,1,0:T(8,128)(2,1)S(1)}, bf16[4,320,128]{2,1,0:T(8,128)(2,1)S(1)}, u32[]{:S(2)}, u32[]{:S(2)}) collective-permute-start(bf16[4,320,128]{2,1,0:T(8,128)(2,1)S(1)} %get-tuple-element.41), channel_id=1, source_target_pairs={{0,2},{2,0},{4,6},{6,4},{8,10},{10,8},{12,14},{14,12},{1,3},{3,1},... | collective-permute-start | bytes 983048 | tf_op jit(solution)/shard_map/ppermute | solution.py:332
  38.1 4.7 %collective-permute-start.3 = (bf16[4,304,128]{2,1,0:T(8,128)(2,1)S(1)}, bf16[4,304,128]{2,1,0:T(8,128)(2,1)S(1)}, u32[]{:S(2)}, u32[]{:S(2)}) collective-permute-start(bf16[4,304,128]{2,1,0:T(8,128)(2,1)S(1)} %get-tuple-element.42), channel_id=1, source_target_pairs={{0,14},{2,4},{4,2},{6,8},{8,6},{10,12},{12,10},{14,0},{1,15},{3,5}... | collective-permute-start | bytes 933896 | tf_op jit(solution)/shard_map/ppermute | solution.py:333
  42.8 7.3 %collective-permute-done.3.second_ref = bf16[4,304,128]{2,1,0:T(8,128)(2,1)S(1)} collective-permute-done((bf16[4,304,128]{2,1,0:T(8,128)(2,1)S(1)}, bf16[4,304,128]{2,1,0:T(8,128)(2,1)S(1)}, u32[]{:S(2)}, u32[]{:S(2)}) %collective-permute-start.3) | collective-permute-done | bytes 311328 | tf_op jit(solution)/shard_map/ppermute | solution.py:333
  50.1 0.0 collective-permute-done.2.first_ref
  50.1 0.7 shard_map.83
  50.8 0.1 collective-permute-start.4
  50.9 3.6 %collective-permute-start.5 = (bf16[624,128]{1,0:T(8,128)(2,1)S(1)}, bf16[624,128]{1,0:T(8,128)(2,1)S(1)}, u32[]{:S(2)}, u32[]{:S(2)}) collective-permute-start(bf16[624,128]{1,0:T(8,128)(2,1)S(1)} %get-tuple-element.45), channel_id=1, source_target_pairs={{0,12},{2,14},{4,0},{6,2},{8,4},{10,6},{12,8},{14,10},{1,13},{3,15... | collective-permute-start | bytes 479240 | tf_op jit(solution)/shard_map/ppermute | solution.py:306
  54.5 3.7 %collective-permute-start.6 = (bf16[624,128]{1,0:T(8,128)(2,1)S(1)}, bf16[624,128]{1,0:T(8,128)(2,1)S(1)}, u32[]{:S(2)}, u32[]{:S(2)}) collective-permute-start(bf16[624,128]{1,0:T(8,128)(2,1)S(1)} %get-tuple-element.46), channel_id=1, source_target_pairs={{0,8},{2,10},{4,12},{6,14},{8,0},{10,2},{12,4},{14,6},{1,9},{3,11}... | collective-permute-start | bytes 479240 | tf_op jit(solution)/shard_map/ppermute | solution.py:306
  58.2 1.4 collective-permute-done.4.up_in
  59.6 7.4 %collective-permute-done.5.down_in = bf16[624,128]{1,0:T(8,128)(2,1)S(1)} collective-permute-done((bf16[624,128]{1,0:T(8,128)(2,1)S(1)}, bf16[624,128]{1,0:T(8,128)(2,1)S(1)}, u32[]{:S(2)}, u32[]{:S(2)}) %collective-permute-start.5) | collective-permute-done | bytes 159776 | tf_op jit(solution)/shard_map/ppermute | solution.py:306
  67.0 0.0 collective-permute-done.6.far_in
  67.0 0.1 shard_map.84
  67.1 0.9 collective-permute-start.7
  68.0 4.7 %collective-permute-start.8 = (bf16[32,128]{1,0:T(8,128)(2,1)S(1)}, bf16[32,128]{1,0:T(8,128)(2,1)S(1)}, u32[]{:S(2)}, u32[]{:S(2)}) collective-permute-start(bf16[32,128]{1,0:T(8,128)(2,1)S(1)} %shard_map.81.refs_0_), channel_id=1, source_target_pairs={{0,2},{2,0},{4,6},{6,4},{8,10},{10,8},{12,14},{14,12},{1,3},{3,1},... | collective-permute-start | bytes 24584 | tf_op jit(solution)/shard_map/ppermute | solution.py:321
  72.7 1.0 collective-permute-done.8.refs_1_
  73.7 2.8 %collective-permute-start.9 = (bf16[32,128]{1,0:T(8,128)(2,1)S(1)}, bf16[32,128]{1,0:T(8,128)(2,1)S(1)}, u32[]{:S(2)}, u32[]{:S(2)}) collective-permute-start(bf16[32,128]{1,0:T(8,128)(2,1)S(1)} %shard_map.85.refs_0_), channel_id=1, source_target_pairs={{0,4},{2,6},{4,8},{6,10},{8,12},{10,14},{12,0},{14,2},{1,5},{3,7},... | collective-permute-start | bytes 24584 | tf_op jit(solution)/shard_map/ppermute | solution.py:306
  76.5 0.8 collective-permute-start.10
  77.3 2.8 %collective-permute-start.11 = (bf16[32,128]{1,0:T(8,128)(2,1)S(1)}, bf16[32,128]{1,0:T(8,128)(2,1)S(1)}, u32[]{:S(2)}, u32[]{:S(2)}) collective-permute-start(bf16[32,128]{1,0:T(8,128)(2,1)S(1)} %shard_map.85.refs_0_), channel_id=1, source_target_pairs={{0,8},{2,10},{4,12},{6,14},{8,0},{10,2},{12,4},{14,6},{1,9},{3,11}... | collective-permute-start | bytes 24584 | tf_op jit(solution)/shard_map/ppermute | solution.py:306
  80.1 0.0 collective-permute-done.9.refs_1_
  80.1 0.0 collective-permute-done.10.refs_2_
  80.1 3.6 %collective-permute-done.11.refs_3_ = bf16[32,128]{1,0:T(8,128)(2,1)S(1)} collective-permute-done((bf16[32,128]{1,0:T(8,128)(2,1)S(1)}, bf16[32,128]{1,0:T(8,128)(2,1)S(1)}, u32[]{:S(2)}, u32[]{:S(2)}) %collective-permute-start.11) | collective-permute-done | bytes 8224 | tf_op jit(solution)/shard_map/ppermute | solution.py:306
  83.7 9.5 %all_to_all.31.parts_ref = bf16[16,32,128]{2,1,0:T(8,128)(2,1)S(1)} all-to-all(bf16[16,32,128]{2,1,0:T(8,128)(2,1)S(1)} %shard_map.86), channel_id=1, replica_groups=mesh['row_0'=4,'row_1'=4,'col_0'=8,'col_1'=2] {'row_0','row_1'}, dimensions={0} | all-to-all | bytes 262144 | tf_op jit(solution)/shard_map/all_to_all | solution.py:29
  93.3 0.0 collective-permute-done.7.arrived_ref
  93.3 0.9 shard_map.88
  94.2 14.8 %all_to_all.32.plane_ref = f32[32,8,128]{2,1,0:T(8,128)S(1)} all-to-all(f32[32,8,128]{2,1,0:T(8,128)S(1)} %get-tuple-element.49), channel_id=1, replica_groups=mesh['row_0'=4,'row_1'=4,'col_0'=8,'col_1'=2] {'row_0','row_1','col_1'}, dimensions={0} | all-to-all | bytes 262144 | tf_op jit(solution)/shard_map/all_to_all | solution.py:29
  109.1 0.1 shard_map.89
  109.1 19.6 %all_to_all.33.ends_ref.hm_ref = bf16[8,224,128]{2,1,0:T(8,128)(2,1)S(1)} all-to-all(bf16[8,224,128]{2,1,0:T(8,128)(2,1)S(1)} %shard_map.89), channel_id=1, replica_groups=mesh['row_0'=4,'row_1'=4,'col_0'=8,'col_1'=2] {'col_0'}, dimensions={0} | all-to-all | bytes 917504 | tf_op jit(solution)/shard_map/all_to_all | solution.py:29
  128.7 0.5 shard_map.90
  129.3 0.0 copy-start.1
  129.3 0.8 copy-done.1
  130.1 0.0 copy-start.7
  130.1 0.8 copy-done.7
  130.8 4.1 %all-to-all-start.4 = ((bf16[8,208,128]{2,1,0:T(8,128)(2,1)}), bf16[8,208,128]{2,1,0:T(8,128)(2,1)}, u32[]{:S(2)}, u32[]{:S(2)}) async-start(bf16[8,208,128]{2,1,0:T(8,128)(2,1)} %copy-done.7), calls=%async_computation.4 | async-start | bytes 851968 | tf_op jit(solution)/shard_map/all_to_all | solution.py:29
  134.9 1.9 %collective-permute-start.13 = (bf16[8,224,128]{2,1,0:T(8,128)(2,1)}, bf16[8,224,128]{2,1,0:T(8,128)(2,1)}, u32[]{:S(2)}, u32[]{:S(2)}) collective-permute-start(bf16[8,224,128]{2,1,0:T(8,128)(2,1)} %copy-done.1), channel_id=1, source_target_pairs={{0,1},{1,0},{2,3},{3,2},{4,5},{5,4},{6,7},{7,6},{8,9},{9,8},{10,11... | collective-permute-start | bytes 1376264 | tf_op jit(solution)/shard_map/ppermute | solution.py:33
  136.9 11.7 %all-to-all-done.4.pm_ref = bf16[8,208,128]{2,1,0:T(8,128)(2,1)} async-done(((bf16[8,208,128]{2,1,0:T(8,128)(2,1)}), bf16[8,208,128]{2,1,0:T(8,128)(2,1)}, u32[]{:S(2)}, u32[]{:S(2)}) %all-to-all-start.4) | async-done | bytes 426016 | tf_op jit(solution)/shard_map/all_to_all | solution.py:29
  148.6 2.7 %collective-permute-start.12 = (bf16[8,208,128]{2,1,0:T(8,128)(2,1)}, bf16[8,208,128]{2,1,0:T(8,128)(2,1)S(1)}, u32[]{:S(2)}, u32[]{:S(2)}) collective-permute-start(bf16[8,208,128]{2,1,0:T(8,128)(2,1)} %all-to-all-done.4.pm_ref), channel_id=1, source_target_pairs={{0,1},{1,0},{2,3},{3,2},{4,5},{5,4},{6,7},{7,6},{8,9},{9,8},{10,11... | collective-permute-start | bytes 1277960 | tf_op jit(solution)/shard_map/ppermute | solution.py:33
  151.3 0.0 collective-permute-done.13.ht_ref
  151.3 1.6 collective-permute-done.12.pt_ref
  152.9 0.0 copy-start.2
  152.9 1.0 copy-done.2
  153.9 0.0 copy-start.6
  153.9 1.0 copy-done.6
  154.9 3.0 %out_terms.1 = bf16[256,1024]{1,0:T(8,128)(2,1)S(1)} custom-call(s32[3]{0:T(128)S(1)} %pad_add_fusion.place_ref, f32[8,128]{1,0:T(8,128)S(1)} %get-tuple-element.54.scale_ref, bf16[8,208,128]{2,1,0:T(8,128)(2,1)S(1)} %collective-permute-done.12.pt_ref, bf16[8,208,128]{2,1,0:T(8,128)(2,1)} %all-to-all-done.4.pm_ref, ...), custom_call_target="tpu_custom_call" | custom-call | flops 872415232 | bytes 3407872 | tf_op jit(solution)/shard_map/out_terms/pallas_call | solution.py:280
  158.0 13.6 %all_to_all.34 = bf16[16,16,1024]{2,1,0:T(8,128)(2,1)S(1)} all-to-all(bf16[16,16,1024]{2,1,0:T(8,128)(2,1)S(1)} %bitcast.7), channel_id=1, replica_groups=mesh['row_0'=4,'row_1'=4,'col_0'=8,'col_1'=2] {'row_0','row_1'}, dimensions={0} | all-to-all | bytes 1048576 | tf_op jit(solution)/shard_map/all_to_all | solution.py:29
  171.5 0.7 reduce_sum.12
  (5 shorter events, 0.0 us)
Async XLA Ops:
  2.1 26.8 %copy-start = (bf16[1664,1024]{1,0:T(8,128)(2,1)S(1)}, bf16[1664,1024]{1,0:T(8,128)(2,1)}, u32[]{:S(2)}) copy-start(bf16[1664,1024]{1,0:T(8,128)(2,1)} %wd_ref.3) | copy-start | bytes 10223620
  2.1 26.8 %copy-start.3 = (bf16[1024,1664]{1,0:T(8,128)(2,1)S(1)}, bf16[1024,1664]{1,0:T(8,128)(2,1)}, u32[]{:S(2)}) copy-start(bf16[1024,1664]{1,0:T(8,128)(2,1)} %wg_ref.1) | copy-start | bytes 10223620
  2.1 26.8 %copy-start.4 = (bf16[1024,1664]{1,0:T(8,128)(2,1)S(1)}, bf16[1024,1664]{1,0:T(8,128)(2,1)}, u32[]{:S(2)}) copy-start(bf16[1024,1664]{1,0:T(8,128)(2,1)} %wu_ref.1) | copy-start | bytes 10223620
  26.9 5.6 %collective-permute-start = (bf16[32,128]{1,0:T(8,128)(2,1)S(1)}, bf16[32,128]{1,0:T(8,128)(2,1)S(1)}, u32[]{:S(2)}, u32[]{:S(2)}) collective-permute-start(bf16[32,128]{1,0:T(8,128)(2,1)S(1)} %get-tuple-element.38), channel_id=1, source_target_pairs={{0,1},{1,0},{2,3},{3,2},{4,5},{5,4},{6,7},{7,6},{8,9},{9,8},{10,11... | collective-permute-start | bytes 24584 | tf_op jit(solution)/shard_map/ppermute | solution.py:33
  32.5 3.9 %copy-start.5 = (bf16[256,1024]{1,0:T(8,128)(2,1)}, bf16[256,1024]{1,0:T(8,128)(2,1)S(1)}, u32[]{:S(2)}) copy-start(bf16[256,1024]{1,0:T(8,128)(2,1)S(1)} %get-tuple-element.56.dy_ref) | copy-start | bytes 1572868
  32.5 3.1 %collective-permute-start.1 = (bf16[8,624,128]{2,1,0:T(8,128)(2,1)S(1)}, bf16[8,624,128]{2,1,0:T(8,128)(2,1)S(1)}, u32[]{:S(2)}, u32[]{:S(2)}) collective-permute-start(bf16[8,624,128]{2,1,0:T(8,128)(2,1)S(1)} %get-tuple-element.39), channel_id=1, source_target_pairs={{0,1},{1,0},{2,3},{3,2},{4,5},{5,4},{6,7},{7,6},{8,9},{9,8},{10,11... | collective-permute-start | bytes 3833864 | tf_op jit(solution)/shard_map/ppermute | solution.py:33
  36.4 13.7 %collective-permute-start.2 = (bf16[4,320,128]{2,1,0:T(8,128)(2,1)S(1)}, bf16[4,320,128]{2,1,0:T(8,128)(2,1)S(1)}, u32[]{:S(2)}, u32[]{:S(2)}) collective-permute-start(bf16[4,320,128]{2,1,0:T(8,128)(2,1)S(1)} %get-tuple-element.41), channel_id=1, source_target_pairs={{0,2},{2,0},{4,6},{6,4},{8,10},{10,8},{12,14},{14,12},{1,3},{3,1},... | collective-permute-start | bytes 983048 | tf_op jit(solution)/shard_map/ppermute | solution.py:332
  38.1 12.0 %collective-permute-start.3 = (bf16[4,304,128]{2,1,0:T(8,128)(2,1)S(1)}, bf16[4,304,128]{2,1,0:T(8,128)(2,1)S(1)}, u32[]{:S(2)}, u32[]{:S(2)}) collective-permute-start(bf16[4,304,128]{2,1,0:T(8,128)(2,1)S(1)} %get-tuple-element.42), channel_id=1, source_target_pairs={{0,14},{2,4},{4,2},{6,8},{8,6},{10,12},{12,10},{14,0},{1,15},{3,5}... | collective-permute-start | bytes 933896 | tf_op jit(solution)/shard_map/ppermute | solution.py:333
  50.8 8.8 %collective-permute-start.4 = (bf16[624,128]{1,0:T(8,128)(2,1)S(1)}, bf16[624,128]{1,0:T(8,128)(2,1)S(1)}, u32[]{:S(2)}, u32[]{:S(2)}) collective-permute-start(bf16[624,128]{1,0:T(8,128)(2,1)S(1)} %get-tuple-element.44), channel_id=1, source_target_pairs={{0,4},{2,6},{4,8},{6,10},{8,12},{10,14},{12,0},{14,2},{1,5},{3,7},... | collective-permute-start | bytes 479240 | tf_op jit(solution)/shard_map/ppermute | solution.py:306
  50.9 16.1 %collective-permute-start.5 = (bf16[624,128]{1,0:T(8,128)(2,1)S(1)}, bf16[624,128]{1,0:T(8,128)(2,1)S(1)}, u32[]{:S(2)}, u32[]{:S(2)}) collective-permute-start(bf16[624,128]{1,0:T(8,128)(2,1)S(1)} %get-tuple-element.45), channel_id=1, source_target_pairs={{0,12},{2,14},{4,0},{6,2},{8,4},{10,6},{12,8},{14,10},{1,13},{3,15... | collective-permute-start | bytes 479240 | tf_op jit(solution)/shard_map/ppermute | solution.py:306
  54.5 12.5 %collective-permute-start.6 = (bf16[624,128]{1,0:T(8,128)(2,1)S(1)}, bf16[624,128]{1,0:T(8,128)(2,1)S(1)}, u32[]{:S(2)}, u32[]{:S(2)}) collective-permute-start(bf16[624,128]{1,0:T(8,128)(2,1)S(1)} %get-tuple-element.46), channel_id=1, source_target_pairs={{0,8},{2,10},{4,12},{6,14},{8,0},{10,2},{12,4},{14,6},{1,9},{3,11}... | collective-permute-start | bytes 479240 | tf_op jit(solution)/shard_map/ppermute | solution.py:306
  67.1 26.2 %collective-permute-start.7 = (bf16[624,128]{1,0:T(8,128)(2,1)S(1)}, bf16[624,128]{1,0:T(8,128)(2,1)S(1)}, u32[]{:S(2)}, u32[]{:S(2)}) collective-permute-start(bf16[624,128]{1,0:T(8,128)(2,1)S(1)} %get-tuple-element.47.acts_ref), channel_id=1, source_target_pairs={{0,1},{1,0},{2,3},{3,2},{4,5},{5,4},{6,7},{7,6},{8,9},{9,8},{10,11... | collective-permute-start | bytes 479240 | tf_op jit(solution)/shard_map/ppermute | solution.py:33
  68.0 5.7 %collective-permute-start.8 = (bf16[32,128]{1,0:T(8,128)(2,1)S(1)}, bf16[32,128]{1,0:T(8,128)(2,1)S(1)}, u32[]{:S(2)}, u32[]{:S(2)}) collective-permute-start(bf16[32,128]{1,0:T(8,128)(2,1)S(1)} %shard_map.81.refs_0_), channel_id=1, source_target_pairs={{0,2},{2,0},{4,6},{6,4},{8,10},{10,8},{12,14},{14,12},{1,3},{3,1},... | collective-permute-start | bytes 24584 | tf_op jit(solution)/shard_map/ppermute | solution.py:321
  73.7 6.4 %collective-permute-start.9 = (bf16[32,128]{1,0:T(8,128)(2,1)S(1)}, bf16[32,128]{1,0:T(8,128)(2,1)S(1)}, u32[]{:S(2)}, u32[]{:S(2)}) collective-permute-start(bf16[32,128]{1,0:T(8,128)(2,1)S(1)} %shard_map.85.refs_0_), channel_id=1, source_target_pairs={{0,4},{2,6},{4,8},{6,10},{8,12},{10,14},{12,0},{14,2},{1,5},{3,7},... | collective-permute-start | bytes 24584 | tf_op jit(solution)/shard_map/ppermute | solution.py:306
  76.5 3.6 %collective-permute-start.10 = (bf16[32,128]{1,0:T(8,128)(2,1)S(1)}, bf16[32,128]{1,0:T(8,128)(2,1)S(1)}, u32[]{:S(2)}, u32[]{:S(2)}) collective-permute-start(bf16[32,128]{1,0:T(8,128)(2,1)S(1)} %shard_map.85.refs_0_), channel_id=1, source_target_pairs={{0,12},{2,14},{4,0},{6,2},{8,4},{10,6},{12,8},{14,10},{1,13},{3,15... | collective-permute-start | bytes 24584 | tf_op jit(solution)/shard_map/ppermute | solution.py:306
  77.3 6.4 %collective-permute-start.11 = (bf16[32,128]{1,0:T(8,128)(2,1)S(1)}, bf16[32,128]{1,0:T(8,128)(2,1)S(1)}, u32[]{:S(2)}, u32[]{:S(2)}) collective-permute-start(bf16[32,128]{1,0:T(8,128)(2,1)S(1)} %shard_map.85.refs_0_), channel_id=1, source_target_pairs={{0,8},{2,10},{4,12},{6,14},{8,0},{10,2},{12,4},{14,6},{1,9},{3,11}... | collective-permute-start | bytes 24584 | tf_op jit(solution)/shard_map/ppermute | solution.py:306
  129.3 0.8 copy-start.1
  130.1 0.8 copy-start.7
  130.8 17.8 %all-to-all-start.4 = ((bf16[8,208,128]{2,1,0:T(8,128)(2,1)}), bf16[8,208,128]{2,1,0:T(8,128)(2,1)}, u32[]{:S(2)}, u32[]{:S(2)}) async-start(bf16[8,208,128]{2,1,0:T(8,128)(2,1)} %copy-done.7), calls=%async_computation.4 | async-start | bytes 851968 | tf_op jit(solution)/shard_map/all_to_all | solution.py:29
  134.9 16.3 %collective-permute-start.13 = (bf16[8,224,128]{2,1,0:T(8,128)(2,1)}, bf16[8,224,128]{2,1,0:T(8,128)(2,1)}, u32[]{:S(2)}, u32[]{:S(2)}) collective-permute-start(bf16[8,224,128]{2,1,0:T(8,128)(2,1)} %copy-done.1), channel_id=1, source_target_pairs={{0,1},{1,0},{2,3},{3,2},{4,5},{5,4},{6,7},{7,6},{8,9},{9,8},{10,11... | collective-permute-start | bytes 1376264 | tf_op jit(solution)/shard_map/ppermute | solution.py:33
  148.6 4.3 %collective-permute-start.12 = (bf16[8,208,128]{2,1,0:T(8,128)(2,1)}, bf16[8,208,128]{2,1,0:T(8,128)(2,1)S(1)}, u32[]{:S(2)}, u32[]{:S(2)}) collective-permute-start(bf16[8,208,128]{2,1,0:T(8,128)(2,1)} %all-to-all-done.4.pm_ref), channel_id=1, source_target_pairs={{0,1},{1,0},{2,3},{3,2},{4,5},{5,4},{6,7},{7,6},{8,9},{9,8},{10,11... | collective-permute-start | bytes 1277960 | tf_op jit(solution)/shard_map/ppermute | solution.py:33
  152.9 1.0 copy-start.2
  153.9 1.0 copy-start.6
